TPU v7x, 256 devices: a whole 4x4x8 slice. The times are simulated.
256 devices in a mesh: rows: 32 (over y, z), cols: 8 (over x, core).
Axes of the slice: x: 4, y: 4, z: 8, core: 2. Of those that a mesh axis runs over, the one named last changes fastest.
Arguments:
- orthophoto: float32 [3, 4096, 4096], P(None, 'rows', 'cols'), may hold values from 0 to 1
Outputs:
- detail_zero: float32 [3, 4096, 4096], P(None, 'rows', 'cols')
- detail_one: float32 [3, 2048, 2048], P(None, 'rows', 'cols')
- detail_two: float32 [3, 1024, 1024], P(None, 'rows', 'cols')
- detail_three: float32 [3, 512, 512], P(None, 'rows', 'cols')
- detail_four: float32 [3, 256, 256], P(None, 'rows', 'cols')
- coarsest: float32 [3, 128, 128], P(None, 'rows', 'cols')
All inputs are finite; a program needn't handle non-finite values.
Results may differ from a plain program's by a relative error of at most 0.00015.
Values sent between devices are 32-bit elements; how exact they have to be, the bound alone decides.
A program may use at most 64 MiB of HBM per device.

v0:
```python
import functools

import jax
import jax.numpy as jnp
import numpy as np
from jax import lax
from jax.experimental import pallas as pl
from jax.experimental.pallas import tpu as pltpu
from jax.sharding import PartitionSpec as P

CH = 3
ROWS = 128
COLS = 512
LEVELS = 5
H = [ROWS >> k for k in range(6)]
W = [COLS >> k for k in range(6)]
R = [0, 72, 40, 24, 16, 8]
BASE = [0, 0, 216, 336, 408, 456]
POS = [0, 0, 0, 0, 64, 96]
F32 = jnp.float32
BF16 = jnp.bfloat16
MESH = pl.DeviceIdType.MESH
TAPS = (1.0, 4.0, 6.0, 4.0, 1.0)


def column_reductions(low, high):
    result = [None]
    total = None
    for k in range(1, LEVELS + 1):
        n = W[k - 1]
        step = np.zeros((n + 3, W[k] + 3))
        for j in range(0 if low else -1, W[k] if high else W[k] + 2):
            for tap in range(5):
                cell = 2 * j - 2 + tap
                if low and cell < 0:
                    cell = -cell
                if high and cell > n - 1:
                    cell = 2 * (n - 1) - cell
                if -1 <= cell <= n + 1:
                    step[cell + 1, j + 1] += TAPS[tap] / 16
        total = step[1 : n + 1] if k == 1 else total @ step
        result.append(total)
    return result


def reduction_table(low, high):
    t = column_reductions(low, high)

    def edge(k):
        cells = (W[k] - 1, W[k] - 1 if high else W[k], W[k] + 1, 1 if low else -1, 0)
        return t[k][:, [c + 1 for c in cells]]

    first = np.zeros((COLS, 512))
    first[:, 0:256] = t[1][:, 1:257]
    first[:, 384:512] = t[2][:, 1:129]
    for k in (1, 2):
        first[:, 256 + 8 * (k - 1) : 256 + 8 * (k - 1) + 5] = edge(k)
    last = np.zeros((COLS, 256))
    for k in (3, 4, 5):
        last[:, 8 * (k - 1) : 8 * (k - 1) + 5] = edge(k)
        last[:, 128 + POS[k] : 128 + POS[k] + W[k]] = t[k][:, 1 : W[k] + 1]
    top = np.asarray(last.astype(jnp.bfloat16), np.float64)
    rest = np.asarray((last - top).astype(jnp.bfloat16), np.float64)
    assert np.array_equal(top + rest, last)
    assert np.array_equal(np.asarray(first.astype(jnp.bfloat16), np.float64), first)
    return np.concatenate([first, top, rest], axis=1)


def expansion_row(k, cell):
    row = np.zeros(2 * W[k])
    for i in range(W[k]):
        row[2 * i] += {i - 1: 0.125, i: 0.75, i + 1: 0.125}.get(cell, 0.0)
        row[2 * i + 1] += {i: 0.5, i + 1: 0.5}.get(cell, 0.0)
    return row


def expansion_table(k, main_at, edge_at, lanes):
    spread = np.zeros((lanes, 2 * W[k]))
    keep = np.zeros((lanes, W[k]))
    for c in range(W[k]):
        spread[main_at + c] = expansion_row(k, c)
        keep[main_at + c, c] = 1
    own = edge_at + 8 * (k - 1)
    came = own + 64
    spread[own + 1] = expansion_row(k, W[k])
    spread[own + 3] = expansion_row(k, -1)
    for s, cell in enumerate((-1, 0, 1, W[k] - 1, W[k])):
        spread[came + s] = expansion_row(k, cell)
        if 0 <= cell < W[k]:
            keep[came + s, cell] = 1
    return spread, keep


def padded(a, cols):
    return np.pad(a, ((0, 0), (0, cols - a.shape[1])))


def tables():
    plain, low, high = (reduction_table(*e) for e in ((False, False), (True, False), (False, True)))
    assert np.array_equal(plain[128:], low[128:]) and np.array_equal(plain[:384], high[:384])
    t_low = np.stack([plain[:128], low[:128]])
    t_high = np.stack([plain[384:], high[384:]])
    v1, s1 = expansion_table(1, 0, 256, 384)
    w2 = np.concatenate(expansion_table(2, 128, 0, 256), axis=1)
    deep = []
    for k in (3, 4, 5):
        spread, keep = expansion_table(k, 128 + POS[k], 0, 256)
        deep.append(np.concatenate([padded(spread, 128), padded(keep, 128)], axis=1))
    return [a.astype(jnp.bfloat16) for a in (t_low, plain[128:384], t_high, v1, s1[256:], w2, np.stack(deep))]


def split3(a):
    top = a.astype(BF16)
    rest = a - top.astype(F32)
    mid = rest.astype(BF16)
    return top, mid, (rest - mid.astype(F32)).astype(BF16)


def dot3(parts, table):
    return sum(jnp.dot(p, table, preferred_element_type=F32) for p in parts)


def reduce_rows(k, src, dst, first, last):
    n, h = H[k - 1], H[k]

    def tap(o):
        return src[:, :, pl.ds(8 + o, h, stride=2), :]

    dst[:, :, 8 : 8 + h, :] = (tap(-2) + tap(2)) * 0.0625 + (tap(-1) + tap(1)) * 0.25 + tap(0) * 0.375

    def s(i):
        return src[:, :, 8 + i : 9 + i, :]

    def d(i):
        return dst[:, :, 8 + i : 9 + i, :]

    below = jnp.where(first, d(1), s(-1) * 0.25 + s(0) * 0.0625)
    zero = jnp.zeros_like(below)
    dst[:, :, 6:7, :] = jnp.where(first, d(2), zero)
    dst[:, :, 7:8, :] = below
    dst[:, :, 8 + h : 9 + h, :] = jnp.where(
        last, d(h - 2), s(n - 2) * 0.0625 + s(n - 1) * 0.25 + s(n) * 0.375 + s(n + 1) * 0.25
    )
    dst[:, :, 9 + h : 10 + h, :] = jnp.where(last, zero, s(n) * 0.0625 + s(n + 1) * 0.25)
    dst[:, :, 10 + h : 11 + h, :] = below
    left = R[k] - h - 3
    dst[:, :, 11 + h : 11 + h + left, :] = jnp.zeros((CH, 4, left, 128), F32)


def rows_of(k, y):
    return jnp.concatenate(
        [jnp.concatenate([y[c, t, 8 : 8 + R[k], :] for t in range(4)], axis=1) for c in range(CH)], axis=0
    )


def kernel(
    x_hbm, tlow_hbm, tmid_hbm, thigh_hbm, v1_hbm, s1_hbm, w2_hbm, w345_hbm,
    o0, o1, o2, o3, o4, o5,
    xs, y1, y2, y3, y4, y5, tv, v1, s1, w2, w345, p1, p2, p3,
    rh, rl, cb, rh_in, rl_in, cbm, cbp, chm, chp, clm, clp,
    g1, g2, g3, g4, g5, m1, m2, m3, m4, d0, d1, d2, d3w, d4w, d3, d4, d5,
    load_sem, out_sem, send_sem, recv_sem,
):
    r, c = lax.axis_index("rows"), lax.axis_index("cols")
    nr, nc = lax.axis_size("rows"), lax.axis_size("cols")
    first, last = r == 0, r == nr - 1
    left, right = c == 0, c == nc - 1
    up, down = jnp.logical_not(first), jnp.logical_not(last)
    west, east = jnp.logical_not(left), jnp.logical_not(right)

    loads = [pltpu.make_async_copy(x_hbm.at[:, :, pl.ds(128 * t, 128)], xs.at[:, t, pl.ds(8, ROWS), :], load_sem.at[t]) for t in range(4)]
    loads += [
        pltpu.make_async_copy(tlow_hbm.at[left.astype(jnp.int32)], tv.at[pl.ds(0, 128)], load_sem.at[4]),
        pltpu.make_async_copy(tmid_hbm, tv.at[pl.ds(128, 256)], load_sem.at[5]),
        pltpu.make_async_copy(thigh_hbm.at[right.astype(jnp.int32)], tv.at[pl.ds(384, 128)], load_sem.at[6]),
        pltpu.make_async_copy(v1_hbm, v1, load_sem.at[7]),
        pltpu.make_async_copy(s1_hbm, s1, load_sem.at[8]),
        pltpu.make_async_copy(w2_hbm, w2, load_sem.at[9]),
        pltpu.make_async_copy(w345_hbm, w345, load_sem.at[10]),
    ]
    for copy in loads:
        copy.start()

    def there(dr, dc):
        ok = jnp.bool_(True)
        if dr:
            ok = jnp.logical_and(ok, up if dr < 0 else down)
        if dc:
            ok = jnp.logical_and(ok, west if dc < 0 else east)
        return ok

    edge = pl.ds(256, 128)
    messages = [
        (rh, rh_in, 1, 0),
        (rl, rl_in, -1, 0),
        (cb, cbm, 0, 1),
        (cb, cbp, 0, -1),
        (rh.at[:, :, edge], chm, 1, 1),
        (rh.at[:, :, edge], chp, 1, -1),
        (rl.at[:, :, edge], clm, -1, 1),
        (rl.at[:, :, edge], clp, -1, -1),
    ]
    barrier = pltpu.get_barrier_semaphore()
    for _, dst, dr, dc in messages:

        @pl.when(there(dr, dc))
        def _(dr=dr, dc=dc):
            pl.semaphore_signal(barrier, inc=1, device_id=(r + dr, c + dc), device_id_type=MESH)

        @pl.when(jnp.logical_not(there(-dr, -dc)))
        def _(dst=dst):
            dst[...] = jnp.zeros_like(dst)

    for copy in loads[:4]:
        copy.wait()
    xs[:, :, 6:7, :] = jnp.where(first, xs[:, :, 10:11, :], 0.0)
    xs[:, :, 7:8, :] = jnp.where(first, xs[:, :, 9:10, :], 0.0)
    xs[:, :, 136:137, :] = jnp.where(last, xs[:, :, 134:135, :], 0.0)
    xs[:, :, 137:138, :] = jnp.zeros((CH, 4, 1, 128), F32)
    ys = (xs, y1, y2, y3, y4, y5)
    for k in range(1, LEVELS + 1):
        reduce_rows(k, ys[k - 1], ys[k], first, last)
    for copy in loads[4:7]:
        copy.wait()
    p1[...] = dot3(split3(rows_of(1, y1)), tv[:, 0:384])
    p2[...] = dot3(split3(rows_of(2, y2)), tv[:, 256:512])
    deep = split3(jnp.concatenate([rows_of(k, ys[k]) for k in (3, 4, 5)], axis=0))
    p3[...] = dot3(deep, tv[:, 512:768]) + dot3(deep, tv[:, 768:1024])

    edges = jnp.concatenate([p1[:, 256:384], p2[:, 0:128], p3[:, 0:128], jnp.zeros((32, 128), F32)], axis=0)
    turned = jnp.transpose(edges)
    place = lax.broadcasted_iota(jnp.int32, (8, 512), 1)

    def of_level(k, a):
        ok = place < (BASE[k + 1] if k < LEVELS else 480)
        return jnp.where(jnp.logical_and(ok, place >= BASE[k]), a, 0.0)

    cb[...] = sum(of_level(k, turned[8 * (k - 1) : 8 * k]) for k in range(1, LEVELS + 1))

    lane = lax.broadcasted_iota(jnp.int32, (1, 128), 1)

    def tiles(k, ch, slot):
        if k == 1:
            at = 72 * ch + slot
            return p1[at : at + 1, 0:256], p1[at : at + 1, 256:384]
        if k == 2:
            at = 40 * ch + slot
            return p2[at : at + 1, 128:256], p2[at : at + 1, 0:128]
        at = BASE[k] - BASE[3] + R[k] * ch + slot
        return p3[at : at + 1, 128:256], p3[at : at + 1, 0:128]

    def strip(ch, slot_of):
        both = [None] + [tiles(k, ch, slot_of(k)) for k in range(1, LEVELS + 1)]
        cells = both[5][1]
        for k in (4, 3, 2, 1):
            cells = jnp.where(lane < 8 * k, both[k][1], cells)
        small = jnp.where(lane < 64, both[3][0], jnp.where(lane < 96, both[4][0], both[5][0]))
        return jnp.concatenate([both[1][0], cells, both[2][0], small], axis=1)

    for ch in range(CH):
        for i in range(3):
            rh[ch, i : i + 1, :] = strip(ch, lambda k: H[k] - 1 + i)
        rl[ch, 0:1, :] = strip(ch, lambda k: H[k] + 2)
        rl[ch, 1:2, :] = strip(ch, lambda k: 0)
        rh[ch, 3:4, :] = jnp.zeros((1, 640), F32)

    neighbours = (up.astype(jnp.int32) + down.astype(jnp.int32) + 1) * (
        west.astype(jnp.int32) + east.astype(jnp.int32) + 1
    ) - 1
    pl.semaphore_wait(barrier, neighbours)
    copies = []
    for m, (src, dst, dr, dc) in enumerate(messages):
        copy = pltpu.make_async_remote_copy(
            src_ref=src, dst_ref=dst, send_sem=send_sem.at[m], recv_sem=recv_sem.at[m],
            device_id=(r + dr, c + dc), device_id_type=MESH,
        )
        copies.append(copy)
        pl.when(there(dr, dc))(copy.start)
    for copy in loads[7:]:
        copy.wait()
    for copy, (_, _, dr, dc) in zip(copies, messages):
        pl.when(there(-dr, -dc))(copy.wait_recv)

    sub = lax.broadcasted_iota(jnp.int32, (8, 512), 0)
    comb = jnp.where(sub < 3, cbm[...], cbp[...])
    came = jnp.transpose(
        jnp.concatenate(
            [jnp.zeros((64, 512), F32)] + [of_level(k, comb) for k in range(1, LEVELS + 1)] + [jnp.zeros((24, 512), F32)],
            axis=0,
        )
    )
    p1[:, 256:384] += came[0:216]
    p2[:, 0:128] += came[216:336]
    p3[:, 0:128] += came[336:480]
    is_left = jnp.bitwise_and(lane, 7) < 3

    def add_row(ch, slot_of, strip_in, corner):
        cells = strip_in[:, 256:384] + pltpu.roll(corner, 64, 1)
        at = 72 * ch + slot_of(1)
        p1[at : at + 1, 0:256] += strip_in[:, 0:256]
        p1[at : at + 1, 256:384] += cells
        at = 40 * ch + slot_of(2)
        p2[at : at + 1, 0:128] += cells
        p2[at : at + 1, 128:256] += strip_in[:, 384:512]
        for k in (3, 4, 5):
            at = BASE[k] - BASE[3] + R[k] * ch + slot_of(k)
            p3[at : at + 1, 0:128] += cells
            p3[at : at + 1, 128:256] += strip_in[:, 512:640]

    for ch in range(CH):
        for i in range(3):
            corner = jnp.where(is_left, chm[ch, i : i + 1, :], chp[ch, i : i + 1, :])
            add_row(ch, lambda k: H[k] + 2 if i == 0 else i - 1, rh_in[ch, i : i + 1, :], corner)
        for i in range(2):
            corner = jnp.where(is_left, clm[ch, i : i + 1, :], clp[ch, i : i + 1, :])
            add_row(ch, lambda k: H[k] - 1 + i, rl_in[ch, i : i + 1, :], corner)

    parts = split3(p1[...])
    wide1 = dot3(parts, v1[...])
    level1 = p1[:, 0:256] + dot3([p[:, 256:384] for p in parts], s1[...])
    both2 = dot3(split3(p2[...]), w2[...])
    deep = p3[...]
    both3 = dot3(split3(deep[0:72]), w345[0])
    both4 = dot3(split3(deep[72:120]), w345[1])
    both5 = dot3(split3(deep[120:144]), w345[2])

    def put(k, wide, g):
        h = H[k]
        for ch in range(CH):
            for t in range(g.shape[1]):
                a = wide[R[k] * ch : R[k] * (ch + 1), 128 * t : 128 * (t + 1)]
                g[ch, t, 8 : 8 + h, :] = a[0:h]
                g[ch, t, 7:8, :] = a[h + 2 : h + 3]
                g[ch, t, 8 + h : 9 + h, :] = jnp.where(last, a[h - 1 : h], a[h : h + 1])

    put(1, wide1, g1)
    put(2, both2[:, 0:256], g2)
    put(3, both3, g3)
    put(4, both4, g4)
    put(5, both5, g5)

    def keep(k, level, m):
        for ch in range(CH):
            for t in range(m.shape[1]):
                m[ch, t] = level[R[k] * ch : R[k] * ch + H[k], 128 * t : 128 * (t + 1)]

    keep(1, level1, m1)
    keep(2, both2[:, 256:384], m2)
    keep(3, both3[:, 128:256], m3)
    keep(4, both4[:, 128:256], m4)

    def detail(k, g, level, at, out):
        h = H[k]
        lo, mid, hi = (g[:, :, 7 + i : 7 + i + h, :] for i in range(3))
        even, odd = pl.ds(at, h, stride=2), pl.ds(at + 1, h, stride=2)
        out[:, :, pl.ds(0, h, stride=2), :] = level[:, :, even, :] - (lo + 6.0 * mid + hi) * 0.125
        out[:, :, pl.ds(1, h, stride=2), :] = level[:, :, odd, :] - (mid + hi) * 0.5

    outs = []

    def send_out(src, dst):
        copy = pltpu.make_async_copy(src, dst, out_sem.at[len(outs)])
        copy.start()
        outs.append(copy)

    detail(1, g1, xs, 8, d0)
    for t in range(4):
        send_out(d0.at[:, t], o0.at[:, :, pl.ds(128 * t, 128)])
    detail(2, g2, m1, 0, d1)
    for t in range(2):
        send_out(d1.at[:, t], o1.at[:, :, pl.ds(128 * t, 128)])
    detail(3, g3, m2, 0, d2)
    send_out(d2.at[:, 0], o2)
    detail(4, g4, m3, 0, d3w)
    d3[...] = d3w[:, 0, :, 0:64]
    send_out(d3, o3)
    detail(5, g5, m4, 0, d4w)
    d4[...] = d4w[:, 0, :, 0:32]
    send_out(d4, o4)
    for ch in range(CH):
        d5[ch] = both5[8 * ch : 8 * ch + 4, 128:144]
    send_out(d5, o5)

    for copy, (_, _, dr, dc) in zip(copies, messages):
        pl.when(there(dr, dc))(copy.wait_send)
    for copy in outs:
        copy.wait()


def body(orthophoto):
    def vmem(*shape, dtype=F32):
        return pltpu.VMEM(shape, dtype)

    scratch = [vmem(CH, 4, ROWS + 16, 128)]
    scratch += [vmem(CH, 4, H[k] + 16, 128) for k in range(1, 6)]
    scratch += [vmem(512, 1024, dtype=BF16), vmem(384, 512, dtype=BF16), vmem(128, 256, dtype=BF16)]
    scratch += [vmem(256, 384, dtype=BF16), vmem(3, 256, 256, dtype=BF16)]
    scratch += [vmem(216, 384), vmem(120, 256), vmem(144, 256)]
    scratch += [vmem(CH, 4, 640), vmem(CH, 2, 640), vmem(8, 512)]
    scratch += [vmem(CH, 4, 640), vmem(CH, 2, 640), vmem(8, 512), vmem(8, 512)]
    scratch += [vmem(CH, 4, 128), vmem(CH, 4, 128), vmem(CH, 2, 128), vmem(CH, 2, 128)]
    scratch += [vmem(CH, t, H[k] + 16, 128) for k, t in ((1, 4), (2, 2), (3, 1), (4, 1), (5, 1))]
    scratch += [vmem(CH, t, H[k], 128) for k, t in ((1, 2), (2, 1), (3, 1), (4, 1))]
    scratch += [vmem(CH, t, H[k], 128) for k, t in ((0, 4), (1, 2), (2, 1), (3, 1), (4, 1))]
    scratch += [vmem(CH, H[3], W[3]), vmem(CH, H[4], W[4]), vmem(CH, H[5], W[5])]
    scratch += [pltpu.SemaphoreType.DMA((n,)) for n in (11, 10, 8, 8)]
    anywhere = pl.BlockSpec(memory_space=pl.ANY)
    results = pl.pallas_call(
        kernel,
        out_shape=[jax.ShapeDtypeStruct((CH, H[k], W[k]), F32) for k in range(6)],
        in_specs=[anywhere] * 8,
        out_specs=[anywhere] * 6,
        scratch_shapes=scratch,
        compiler_params=pltpu.CompilerParams(collective_id=0, has_side_effects=True),
    )(orthophoto, *tables())
    return tuple(results)


def solution(mesh):
    placed = P(None, "rows", "cols")
    return jax.shard_map(body, mesh=mesh, in_specs=(placed,), out_specs=(placed,) * 6, check_vma=False)
```

profile of v0, /device:TPU:25, one launch (start us, length us, event | category | flops | bytes accessed | tf_op | source)
XLA Modules:
  0.0 20.7 jit_solution(12287508819328690713)
XLA Ops:
  0.6 14.4 %shard_map.127 = (f32[3,128,512]{2,1,0:T(8,128)}, f32[3,64,256]{2,1,0:T(8,128)}, f32[3,32,128]{2,1,0:T(8,128)}, f32[3,16,64]{2,1,0:T(8,128)}, f32[3,8,32]{2,1,0:T(8,128)}, /*index=5*/f32[3,4,16]{2,1,0:T(4,128)}) custom-call(f32[3,128,512]{2,1,0:T(8,128)} %x_hbm.1, bf16[2,128,1024]{2,1,0:T(8,128)(2,1)} %constant.14.clone.tlow_hbm, ...), custom_call_target="tpu_custom_call" | custom-call | tf_op jit(solution)/shard_map/pallas_call | solution.py:408
  15.0 0.0 copy-start
  15.0 2.1 %copy.20 = f32[3,128,512]{2,1,0:T(8,128)} copy(f32[3,128,512]{2,1,0:T(8,128)} %get-tuple-element.12) | data formatting | bytes 1572864
  17.1 0.0 copy-done
  17.1 0.0 copy-start.1
  17.1 0.7 %copy.21 = f32[3,64,256]{2,1,0:T(8,128)} copy(f32[3,64,256]{2,1,0:T(8,128)S(1)} %copy-done) | data formatting | bytes 393216
  17.8 0.1 copy-done.1
  17.9 0.0 copy-start.2
  17.9 0.6 %copy.22 = f32[3,32,128]{2,1,0:T(8,128)} copy(f32[3,32,128]{2,1,0:T(8,128)S(1)} %copy-done.1) | data formatting | bytes 98304
  18.5 0.1 copy-done.2
  18.7 0.0 copy-start.3
  18.7 0.6 %copy.23 = f32[3,16,64]{2,1,0:T(8,128)} copy(f32[3,16,64]{2,1,0:T(8,128)S(1)} %copy-done.2) | data formatting | bytes 24576
  19.3 0.1 copy-done.3
  19.4 0.0 copy-start.4
  19.4 0.6 %copy.24 = f32[3,8,32]{2,1,0:T(8,128)} copy(f32[3,8,32]{2,1,0:T(8,128)S(1)} %copy-done.3) | data formatting | bytes 6144
  20.0 0.1 copy-done.4
  20.1 0.6 %copy.25 = f32[3,4,16]{2,1,0:T(4,128)} copy(f32[3,4,16]{2,1,0:T(4,128)S(1)} %copy-done.4) | data formatting | bytes 1536
Async XLA Ops:
  15.0 2.1 %copy-start = (f32[3,64,256]{2,1,0:T(8,128)S(1)}, f32[3,64,256]{2,1,0:T(8,128)}, u32[]{:S(2)}) copy-start(f32[3,64,256]{2,1,0:T(8,128)} %get-tuple-element.13) | copy-start | bytes 589828
  17.1 0.8 %copy-start.1 = (f32[3,32,128]{2,1,0:T(8,128)S(1)}, f32[3,32,128]{2,1,0:T(8,128)}, u32[]{:S(2)}) copy-start(f32[3,32,128]{2,1,0:T(8,128)} %get-tuple-element.14) | copy-start | bytes 147460
  17.9 0.7 %copy-start.2 = (f32[3,16,64]{2,1,0:T(8,128)S(1)}, f32[3,16,64]{2,1,0:T(8,128)}, u32[]{:S(2)}) copy-start(f32[3,16,64]{2,1,0:T(8,128)} %get-tuple-element.15) | copy-start | bytes 36868
  18.7 0.7 %copy-start.3 = (f32[3,8,32]{2,1,0:T(8,128)S(1)}, f32[3,8,32]{2,1,0:T(8,128)}, u32[]{:S(2)}) copy-start(f32[3,8,32]{2,1,0:T(8,128)} %get-tuple-element.16) | copy-start | bytes 9220
  19.4 0.7 %copy-start.4 = (f32[3,4,16]{2,1,0:T(4,128)S(1)}, f32[3,4,16]{2,1,0:T(4,128)}, u32[]{:S(2)}) copy-start(f32[3,4,16]{2,1,0:T(4,128)} %get-tuple-element.17) | copy-start | bytes 2308
where the time goes:
time: 21 us; the launch traced here: 20.7 us
  Pallas kernels  14.4 us (69%)
  local copies, waits for them, and re-layouts  5.65 us (27%)
  between operations  0.65 us (3%)
    pallas_call x1, Pallas kernels, body(): pl.pallas_call(kernel, out_shape=[jax.ShapeDtypeStruct((CH, H[k], W[k]),...  14.4 us
    unnamed x16, local copies, waits for them, and re-layouts  5.65 us

commit v1 on v0

--- a/solution.py
+++ b/solution.py
@@ -153,13 +153,12 @@
     )
 
 
-def kernel(
+def exchange_kernel(
     x_hbm, tlow_hbm, tmid_hbm, thigh_hbm, v1_hbm, s1_hbm, w2_hbm, w345_hbm,
-    o0, o1, o2, o3, o4, o5,
-    xs, y1, y2, y3, y4, y5, tv, v1, s1, w2, w345, p1, p2, p3,
+    xs, g1, g2, g3, g4, g5, m1, m2, m3, m4, m5,
+    y1, y2, y3, y4, y5, tv, v1, s1, w2, w345, p1, p2, p3,
     rh, rl, cb, rh_in, rl_in, cbm, cbp, chm, chp, clm, clp,
-    g1, g2, g3, g4, g5, m1, m2, m3, m4, d0, d1, d2, d3w, d4w, d3, d4, d5,
-    load_sem, out_sem, send_sem, recv_sem,
+    load_sem, send_sem, recv_sem,
 ):
     r, c = lax.axis_index("rows"), lax.axis_index("cols")
     nr, nc = lax.axis_size("rows"), lax.axis_size("cols")
@@ -349,6 +348,17 @@
     keep(3, both3[:, 128:256], m3)
     keep(4, both4[:, 128:256], m4)
 
+    for ch in range(CH):
+        m5[ch] = both5[8 * ch : 8 * ch + 8, 128:256]
+    for copy, (_, _, dr, dc) in zip(copies, messages):
+        pl.when(there(dr, dc))(copy.wait_send)
+
+
+def detail_kernel(
+    xs, g1, g2, g3, g4, g5, m1, m2, m3, m4, m5,
+    o0, o1, o2, o3, o4, o5,
+    d0, d1, d2, d3w, d4w, d3, d4, d5, out_sem,
+):
     def detail(k, g, level, at, out):
         h = H[k]
         lo, mid, hi = (g[:, :, 7 + i : 7 + i + h, :] for i in range(3))
@@ -377,12 +387,9 @@
     detail(5, g5, m4, 0, d4w)
     d4[...] = d4w[:, 0, :, 0:32]
     send_out(d4, o4)
-    for ch in range(CH):
-        d5[ch] = both5[8 * ch : 8 * ch + 4, 128:144]
+    d5[...] = m5[:, 0:4, 0:16]
     send_out(d5, o5)
 
-    for copy, (_, _, dr, dc) in zip(copies, messages):
-        pl.when(there(dr, dc))(copy.wait_send)
     for copy in outs:
         copy.wait()
 
@@ -391,28 +398,37 @@
     def vmem(*shape, dtype=F32):
         return pltpu.VMEM(shape, dtype)
 
-    scratch = [vmem(CH, 4, ROWS + 16, 128)]
-    scratch += [vmem(CH, 4, H[k] + 16, 128) for k in range(1, 6)]
+    held = [(CH, 4, ROWS + 16, 128)]
+    held += [(CH, t, H[k] + 16, 128) for k, t in ((1, 4), (2, 2), (3, 1), (4, 1), (5, 1))]
+    held += [(CH, t, H[k], 128) for k, t in ((1, 2), (2, 1), (3, 1), (4, 1))] + [(CH, 8, 128)]
+    scratch = [vmem(CH, 4, H[k] + 16, 128) for k in range(1, 6)]
     scratch += [vmem(512, 1024, dtype=BF16), vmem(384, 512, dtype=BF16), vmem(128, 256, dtype=BF16)]
     scratch += [vmem(256, 384, dtype=BF16), vmem(3, 256, 256, dtype=BF16)]
     scratch += [vmem(216, 384), vmem(120, 256), vmem(144, 256)]
     scratch += [vmem(CH, 4, 640), vmem(CH, 2, 640), vmem(8, 512)]
     scratch += [vmem(CH, 4, 640), vmem(CH, 2, 640), vmem(8, 512), vmem(8, 512)]
     scratch += [vmem(CH, 4, 128), vmem(CH, 4, 128), vmem(CH, 2, 128), vmem(CH, 2, 128)]
-    scratch += [vmem(CH, t, H[k] + 16, 128) for k, t in ((1, 4), (2, 2), (3, 1), (4, 1), (5, 1))]
-    scratch += [vmem(CH, t, H[k], 128) for k, t in ((1, 2), (2, 1), (3, 1), (4, 1))]
-    scratch += [vmem(CH, t, H[k], 128) for k, t in ((0, 4), (1, 2), (2, 1), (3, 1), (4, 1))]
+    scratch += [pltpu.SemaphoreType.DMA((n,)) for n in (11, 8, 8)]
+    anywhere = pl.BlockSpec(memory_space=pltpu.HBM)
+    inside = pl.BlockSpec(memory_space=pltpu.VMEM)
+    arrays = pl.pallas_call(
+        exchange_kernel,
+        out_shape=[jax.ShapeDtypeStruct(shape, F32) for shape in held],
+        in_specs=[anywhere] * 8,
+        out_specs=[inside] * len(held),
+        scratch_shapes=scratch,
+        compiler_params=pltpu.CompilerParams(collective_id=0, has_side_effects=True, vmem_limit_bytes=24 << 20),
+    )(*[pltpu.with_memory_space_constraint(jnp.asarray(a), pltpu.HBM) for a in (orthophoto, *tables())])
+    scratch = [vmem(CH, t, H[k], 128) for k, t in ((0, 4), (1, 2), (2, 1), (3, 1), (4, 1))]
     scratch += [vmem(CH, H[3], W[3]), vmem(CH, H[4], W[4]), vmem(CH, H[5], W[5])]
-    scratch += [pltpu.SemaphoreType.DMA((n,)) for n in (11, 10, 8, 8)]
-    anywhere = pl.BlockSpec(memory_space=pl.ANY)
     results = pl.pallas_call(
-        kernel,
+        detail_kernel,
         out_shape=[jax.ShapeDtypeStruct((CH, H[k], W[k]), F32) for k in range(6)],
-        in_specs=[anywhere] * 8,
+        in_specs=[inside] * len(held),
         out_specs=[anywhere] * 6,
-        scratch_shapes=scratch,
-        compiler_params=pltpu.CompilerParams(collective_id=0, has_side_effects=True),
-    )(orthophoto, *tables())
+        scratch_shapes=scratch + [pltpu.SemaphoreType.DMA((10,))],
+        compiler_params=pltpu.CompilerParams(vmem_limit_bytes=8 << 20),
+    )(*arrays)
     return tuple(results)
 
 

time: 21 us -> 15.3 us (0.73)
  local copies, waits for them, and re-layouts: 5.65 us -> 0 us
    unnamed x16 -> x0, local copies, waits for them, and re-layouts: 5.65 us -> none
    pallas_call x1 -> x2, Pallas kernels: 14.4 us -> 14.5 us  [the longest x1 13.2 us: body(): pl.pallas_call(exchange_kernel, out_shape=[jax.ShapeDtypeStruct(shape, F3...]
where the time goes in v1:
time: 15.3 us; the launch traced here: 15.2 us
  Pallas kernels  14.5 us (95%)
  between operations  0.64 us (4%)
    pallas_call x1, Pallas kernels, body(): pl.pallas_call(exchange_kernel, out_shape=[jax.ShapeDtypeStruct(shape, F3...  13.2 us
    pallas_call x1, Pallas kernels, body(): pl.pallas_call(detail_kernel, out_shape=[jax.ShapeDtypeStruct((CH, H[k],...  1.29 us

profile of v1, /device:TPU:25, one launch (start us, length us, event | category | flops | bytes accessed | tf_op | source)
XLA Modules:
  0.0 15.2 jit_solution(13548377016750176552)
XLA Ops:
  0.6 13.2 %shard_map.127 = (f32[3,4,144,128]{3,2,1,0:T(8,128)S(1)}, f32[3,4,80,128]{3,2,1,0:T(8,128)S(1)}, f32[3,2,48,128]{3,2,1,0:T(8,128)S(1)}, f32[3,1,32,128]{3,2,1,0:...) custom-call(f32[3,128,512]{2,1,0:T(8,128)} %x_hbm.1, ...), custom_call_target="tpu_custom_call" | custom-call | tf_op jit(solution)/shard_map/pallas_call | solution.py:414
  13.9 1.3 %shard_map.128 = (f32[3,128,512]{2,1,0:T(8,128)}, f32[3,64,256]{2,1,0:T(8,128)}, f32[3,32,128]{2,1,0:T(8,128)}, f32[3,16,64]{2,1,0:T(8,128)}, f32[3,8,32]{2,1,0:T(8,128)}, /*index=5*/f32[3,4,16]{2,1,0:T(4,128)}) custom-call(f32[3,4,144,128]{3,2,1,0:T(8,128)S(1)} %get-tuple-element.17.xs, f32[3,4,80,128]{3,2,1,0:T(8,128)S(1)} %get-tuple-element.18.g1, ...), custom_call_target="tpu_custom_call" | custom-call | tf_op jit(solution)/shard_map/pallas_call | solution.py:424

commit v2 on v1

v2 whole, which is shorter than its diff:
```python
import functools

import jax
import jax.numpy as jnp
import numpy as np
from jax import lax
from jax.experimental import pallas as pl
from jax.experimental.pallas import tpu as pltpu
from jax.sharding import PartitionSpec as P

CH = 3
ROWS = 128
COLS = 512
LEVELS = 5
H = [ROWS >> k for k in range(6)]
W = [COLS >> k for k in range(6)]
R = [0, 72, 40, 24, 16, 8]
BASE = [0, 0, 216, 336, 408, 456]
POS = [0, 0, 0, 0, 64, 96]
F32 = jnp.float32
BF16 = jnp.bfloat16
MESH = pl.DeviceIdType.MESH
TAPS = (1.0, 4.0, 6.0, 4.0, 1.0)


def column_reductions(low, high):
    result = [None]
    total = None
    for k in range(1, LEVELS + 1):
        n = W[k - 1]
        step = np.zeros((n + 3, W[k] + 3))
        for j in range(0 if low else -1, W[k] if high else W[k] + 2):
            for tap in range(5):
                cell = 2 * j - 2 + tap
                if low and cell < 0:
                    cell = -cell
                if high and cell > n - 1:
                    cell = 2 * (n - 1) - cell
                if -1 <= cell <= n + 1:
                    step[cell + 1, j + 1] += TAPS[tap] / 16
        total = step[1 : n + 1] if k == 1 else total @ step
        result.append(total / 16.0**k)
    return result


def reduction_table(low, high):
    t = column_reductions(low, high)

    def edge(k):
        cells = (W[k] - 1, W[k] - 1 if high else W[k], W[k] + 1, 1 if low else -1, 0)
        return t[k][:, [c + 1 for c in cells]]

    first = np.zeros((COLS, 512))
    first[:, 0:256] = t[1][:, 1:257]
    first[:, 384:512] = t[2][:, 1:129]
    last = np.zeros((COLS, 256))
    for k in (3, 4, 5):
        last[:, 8 * (k - 1) : 8 * (k - 1) + 5] = edge(k)
        last[:, 128 + POS[k] : 128 + POS[k] + W[k]] = t[k][:, 1 : W[k] + 1]
    for k in (1, 2):
        first[:, 256 + 8 * (k - 1) : 256 + 8 * (k - 1) + 5] = edge(k)
    top = np.asarray(last.astype(jnp.bfloat16), np.float64)
    rest = np.asarray((last - top).astype(jnp.bfloat16), np.float64)
    assert np.array_equal(top + rest, last)
    first[:, 272:296] = top[:, 16:40]
    assert np.array_equal(np.asarray(first.astype(jnp.bfloat16), np.float64), first)
    return np.concatenate([first, top, rest], axis=1)


def expansion_row(k, cell):
    row = np.zeros(2 * W[k])
    for i in range(W[k]):
        row[2 * i] += {i - 1: 0.125, i: 0.75, i + 1: 0.125}.get(cell, 0.0)
        row[2 * i + 1] += {i: 0.5, i + 1: 0.5}.get(cell, 0.0)
    return row


def expansion_table(k, main_at, edge_at, lanes):
    spread = np.zeros((lanes, 2 * W[k]))
    keep = np.zeros((lanes, W[k]))
    for c in range(W[k]):
        spread[main_at + c] = expansion_row(k, c)
        keep[main_at + c, c] = 1
    own = edge_at + 8 * (k - 1)
    came = own + 64
    spread[own + 1] = expansion_row(k, W[k])
    spread[own + 3] = expansion_row(k, -1)
    for s, cell in enumerate((-1, 0, 1, W[k] - 1, W[k])):
        spread[came + s] = expansion_row(k, cell)
        if 0 <= cell < W[k]:
            keep[came + s, cell] = 1
    return spread, keep


def arrival_table(k):
    spread = np.zeros((128, 2 * W[k]))
    keep = np.zeros((128, W[k]))
    for part in range(3):
        for s, cell in enumerate((-1, 0, 1, W[k] - 1, W[k])):
            lane = 24 * (k - 1) + 8 * part + s
            spread[lane] = expansion_row(k, cell)
            if 0 <= cell < W[k]:
                keep[lane, cell] = 1
    return spread, keep


def padded(a, cols):
    return np.pad(a, ((0, 0), (0, cols - a.shape[1])))


def tables():
    plain, low, high = (reduction_table(*e) for e in ((False, False), (True, False), (False, True)))
    assert np.array_equal(plain[128:], low[128:]) and np.array_equal(plain[:384], high[:384])
    t_low = np.stack([plain[:128], low[:128]])
    t_high = np.stack([plain[384:], high[384:]])
    v1, s1 = expansion_table(1, 0, 256, 384)
    w2 = np.concatenate(expansion_table(2, 128, 0, 256), axis=1)
    deep = []
    for k in (3, 4, 5):
        spread, keep = expansion_table(k, 128 + POS[k], 0, 256)
        deep.append(np.concatenate([padded(spread, 128), padded(keep, 128)], axis=1))
    spread, keep = arrival_table(1)
    assert not spread[:, 128:384].any()
    arrive = [spread[:, :128], spread[:, 384:], keep]
    arrive += arrival_table(2)
    for k in (3, 4, 5):
        arrive += [padded(a, 128) for a in arrival_table(k)]
    parts = (t_low, plain[128:384], t_high, v1, s1[256:], w2, np.stack(deep), np.concatenate(arrive, axis=1))
    return [a.astype(jnp.bfloat16) for a in parts]


def split3(a):
    top = a.astype(BF16)
    rest = a - top.astype(F32)
    mid = rest.astype(BF16)
    return top, mid, (rest - mid.astype(F32)).astype(BF16)


def dot3(a, table):
    m = a.shape[0]
    p = jnp.dot(jnp.concatenate(split3(a), axis=0), table, preferred_element_type=F32)
    return p[0:m] + p[m : 2 * m] + p[2 * m : 3 * m]


def reduce_rows(k, t, src, dst, first, last):
    h = H[k]
    count = R[k]

    def tap(o):
        return src[:, t, pl.ds(6 + o, count, stride=2), :]

    dst[:, t, 7 : 7 + count, :] = (tap(-2) + tap(2)) + (tap(-1) + tap(1)) * 4.0 + tap(0) * 6.0
    mirror(dst, t, h, first, last, k < LEVELS)


def mirror(a, t, h, first, last, outer):
    a[:, t, 7:8, :] = a[:, t, pl.ds(jnp.where(first, 9, 7), 1), :]
    if outer:
        a[:, t, 6:7, :] = a[:, t, pl.ds(jnp.where(first, 10, 6), 1), :]
        a[:, t, 8 + h : 9 + h, :] = a[:, t, pl.ds(jnp.where(last, 6 + h, 8 + h), 1), :]


def rows_of(k, y, tiles):
    return jnp.concatenate(
        [jnp.concatenate([y[c, t, 7 : 7 + R[k], :] for t in tiles], axis=1) for c in range(CH)], axis=0
    )


def detail(g, level, at, out, count):
    lo, mid, hi = (g[:, :, i : i + count, :] for i in range(3))
    even, odd = pl.ds(at, count, stride=2), pl.ds(at + 1, count, stride=2)
    out[:, :, pl.ds(0, count, stride=2), :] = level[:, :, even, :] - ((lo + hi) * 0.125 + mid * 0.75)
    out[:, :, pl.ds(1, count, stride=2), :] = level[:, :, odd, :] - (mid + hi) * 0.5


def exchange_kernel(
    x_hbm, tlow_hbm, tmid_hbm, thigh_hbm, v1_hbm, s1_hbm, w2_hbm, w345_hbm, arrive_hbm,
    d0, d1, d2, d3, d4, d5,
    xs, y1, y2, y3, y4, y5, tv, v1, s1, w2, w345, arrive, srs, ri, ci,
    rh, rl, cb, rh_in, rl_in, cbm, cbp, chm, chp, clm, clp,
    g1, g2, g3, g4, g5, m1, m2, m3, m4, m5, d3w, d4w,
    load_sem, send_sem, recv_sem,
):
    r, c = lax.axis_index("rows"), lax.axis_index("cols")
    nr, nc = lax.axis_size("rows"), lax.axis_size("cols")
    first, last = r == 0, r == nr - 1
    left, right = c == 0, c == nc - 1
    up, down = jnp.logical_not(first), jnp.logical_not(last)
    west, east = jnp.logical_not(left), jnp.logical_not(right)

    loads = [
        pltpu.make_async_copy(x_hbm.at[:, :, pl.ds(128 * t, 128)], xs.at[:, t, pl.ds(8, ROWS), :], load_sem.at[t])
        for t in range(4)
    ]
    loads += [
        pltpu.make_async_copy(tlow_hbm.at[left.astype(jnp.int32)], tv.at[pl.ds(0, 128)], load_sem.at[4]),
        pltpu.make_async_copy(tmid_hbm, tv.at[pl.ds(128, 256)], load_sem.at[5]),
        pltpu.make_async_copy(thigh_hbm.at[right.astype(jnp.int32)], tv.at[pl.ds(384, 128)], load_sem.at[6]),
        pltpu.make_async_copy(v1_hbm, v1, load_sem.at[7]),
        pltpu.make_async_copy(s1_hbm, s1, load_sem.at[8]),
        pltpu.make_async_copy(w2_hbm, w2, load_sem.at[9]),
        pltpu.make_async_copy(w345_hbm, w345, load_sem.at[10]),
        pltpu.make_async_copy(arrive_hbm, arrive, load_sem.at[11]),
    ]
    for copy in loads:
        copy.start()

    def there(dr, dc):
        ok = jnp.bool_(True)
        if dr:
            ok = jnp.logical_and(ok, up if dr < 0 else down)
        if dc:
            ok = jnp.logical_and(ok, west if dc < 0 else east)
        return ok

    edge = pl.ds(256, 128)
    messages = [
        (rh, rh_in, 1, 0),
        (rh.at[:, :, edge], chm, 1, 1),
        (rh.at[:, :, edge], chp, 1, -1),
        (rl, rl_in, -1, 0),
        (rl.at[:, :, edge], clm, -1, 1),
        (rl.at[:, :, edge], clp, -1, -1),
        (cb, cbm, 0, 1),
        (cb, cbp, 0, -1),
    ]
    barrier = pltpu.get_barrier_semaphore()
    for _, dst, dr, dc in messages:

        @pl.when(there(dr, dc))
        def _(dr=dr, dc=dc):
            pl.semaphore_signal(barrier, inc=1, device_id=(r + dr, c + dc), device_id_type=MESH)

        @pl.when(jnp.logical_not(there(-dr, -dc)))
        def _(dst=dst):
            dst[...] = jnp.zeros_like(dst)

    ys = (xs, y1, y2, y3, y4, y5)
    for k in range(LEVELS):
        ys[k][:, :, 0:8, :] = jnp.zeros((CH, 4, 8, 128), F32)
        ys[k][:, :, 8 + H[k] : 32 + H[k], :] = jnp.zeros((CH, 4, 24, 128), F32)
    srs[...] = jnp.zeros_like(srs)
    ri[...] = jnp.zeros_like(ri)
    ci[...] = jnp.zeros_like(ci)
    rh[...] = jnp.zeros_like(rh)

    for t in range(4):
        loads[t].wait()
        mirror(xs, t, ROWS, first, last, True)
        for k in range(1, LEVELS + 1):
            reduce_rows(k, t, ys[k - 1], ys[k], first, last)

    for k in range(1, LEVELS + 1):
        for ch in range(CH):
            at = 16 * (k - 1) + 3 * ch
            srs[:, at : at + 3, :] = ys[k][ch, :, 7 + H[k] : 10 + H[k], :]
            at = 16 * (k - 1) + 9 + 2 * ch
            srs[:, at : at + 2, :] = ys[k][ch, :, 7:9, :]
    for copy in loads[4:7]:
        copy.wait()
    strips = jnp.concatenate([srs[t] for t in range(4)], axis=1)
    near = dot3(strips[0:32], tv[:, 0:512])
    deep = dot3(strips[32:80], tv[:, 512:1024])
    deep = deep[:, 0:256] + deep[:, 256:512]
    lane = lax.broadcasted_iota(jnp.int32, (16, 128), 1)
    cells = jnp.where(lane < 32, deep[16:32, 0:128], deep[32:48, 0:128])
    cells = jnp.where(lane < 24, deep[0:16, 0:128], cells)
    cells = jnp.where(lane < 8, near[0:16, 256:384], jnp.where(lane < 16, near[16:32, 256:384], cells))
    small = jnp.where(lane < 64, deep[0:16, 128:256], jnp.where(lane < 96, deep[16:32, 128:256], deep[32:48, 128:256]))
    strips = jnp.concatenate([near[0:16, 0:256], cells, near[16:32, 384:512], small], axis=1)
    for ch in range(CH):
        rh[ch, 0:3, :] = strips[3 * ch : 3 * ch + 3]
        rl[ch, :, :] = strips[9 + 2 * ch : 11 + 2 * ch]

    neighbours = (up.astype(jnp.int32) + down.astype(jnp.int32) + 1) * (
        west.astype(jnp.int32) + east.astype(jnp.int32) + 1
    ) - 1
    pl.semaphore_wait(barrier, neighbours)
    copies = []
    for m, (src, dst, dr, dc) in enumerate(messages):
        copies.append(
            pltpu.make_async_remote_copy(
                src_ref=src, dst_ref=dst, send_sem=send_sem.at[m], recv_sem=recv_sem.at[m],
                device_id=(r + dr, c + dc), device_id_type=MESH,
            )
        )
        if m < 6:
            pl.when(there(dr, dc))(copies[m].start)

    outer = jnp.concatenate([rows_of(k, ys[k], (0, 3)) for k in range(1, LEVELS + 1)], axis=0)
    table = jnp.concatenate([tv[0:128], tv[384:512]], axis=0)
    turned = dot3(outer, jnp.concatenate([table[:, 256:384], table[:, 768:896]], axis=1))
    turned = jnp.concatenate([turned[:, 0:128] + turned[:, 128:256], jnp.zeros((32, 128), F32)], axis=0)
    turned = jnp.transpose(turned)
    place = lax.broadcasted_iota(jnp.int32, (8, 512), 1)

    def of_level(k, a):
        ok = place < (BASE[k + 1] if k < LEVELS else 480)
        return jnp.where(jnp.logical_and(ok, place >= BASE[k]), a, 0.0)

    cb[...] = sum(of_level(k, turned[8 * (k - 1) : 8 * k]) for k in range(1, LEVELS + 1))
    for m in (6, 7):
        pl.when(there(*messages[m][2:]))(copies[m].start)

    for copy in loads[7:]:
        copy.wait()
    p12 = dot3(jnp.concatenate([rows_of(k, ys[k], range(4)) for k in (1, 2)], axis=0), tv[:, 0:512])
    p345 = dot3(jnp.concatenate([rows_of(k, ys[k], range(4)) for k in (3, 4, 5)], axis=0), tv[:, 512:1024])
    p345 = p345[:, 0:256] + p345[:, 256:512]

    def put(k, a, out):
        for ch in range(CH):
            for t in range(out.shape[1]):
                out[ch, t] = a[R[k] * ch : R[k] * (ch + 1), 128 * t : 128 * (t + 1)]

    put(1, dot3(p12[0:224, 0:384], v1[...]), g1)
    put(1, p12, m1)
    both = dot3(p12[208:336, 256:512], w2[...])
    put(2, both[8:, 0:256], g2)
    put(2, both[8:, 256:384], m2)
    deeper = ((3, 0, g3, m3), (4, 72, g4, m4), (5, 112, g5, m5))
    for k, at, g, m in deeper:
        both = dot3(p345[at : at + 16 * -(-3 * R[k] // 16)], w345[k - 3])
        skip = BASE[k] - BASE[3] - at
        put(k, both[skip:, 0:128], g)
        put(k, both[skip:, 128:256], m)

    def add(k, a, out, tiles, first_tile=0):
        for ch in range(CH):
            for i, t in enumerate(tiles):
                lanes = 128 * (first_tile + i)
                out[ch, t] += a[R[k] * ch : R[k] * (ch + 1), lanes : lanes + 128]

    for m in (6, 7):
        pl.when(there(-messages[m][2], -messages[m][3]))(copies[m].wait_recv)
    sub = lax.broadcasted_iota(jnp.int32, (8, 512), 0)
    terms = [a.astype(F32) for a in split3(jnp.where(sub < 3, cbm[...], cbp[...]))]
    came = jnp.concatenate(
        [of_level(k, a) for k in range(1, LEVELS + 1) for a in terms] + [jnp.zeros((8, 512), F32)], axis=0
    )
    came = jnp.transpose(came)

    def arrived(k, at, rows, lanes, count):
        return jnp.dot(
            came[at : at + rows].astype(BF16), arrive[:, lanes : lanes + count], preferred_element_type=F32
        )[BASE[k] - at :]

    more = arrived(1, 0, 224, 0, 512)
    add(1, more, g1, (0, 3))
    add(1, more, m1, (0, 1), 2)
    more = arrived(2, 208, 128, 512, 384)
    add(2, more, g2, (0, 1))
    add(2, more, m2, (0,), 2)
    for k, at, g, m in deeper:
        more = arrived(k, BASE[3] + at, 16 * -(-3 * R[k] // 16), 896 + 256 * (k - 3), 256)
        add(k, more, g, (0,))
        add(k, more, m, (0,), 1)

    side = jnp.bitwise_and(lax.broadcasted_iota(jnp.int32, (1, 128), 1), 7) < 3

    def add_rows(strip, minus, plus, count, row_of):
        for ch in range(CH):
            ri[count * ch : count * (ch + 1), :] = strip[ch, 0:count, :]
            ci[count * ch : count * (ch + 1), :] = jnp.where(side, minus[ch, 0:count, :], plus[ch, 0:count, :])
        strips = ri[...]
        cells = strips[:, 256:384] + pltpu.roll(ci[...], 64, 1)
        wide = dot3(jnp.concatenate([strips[:, 0:256], cells], axis=1), v1[...])
        level = strips[:, 0:256] + dot3(cells, s1[...])
        both = [dot3(jnp.concatenate([cells, strips[:, 384:512]], axis=1), w2[...])]
        tail = jnp.concatenate([cells, strips[:, 512:640]], axis=1)
        both += [dot3(tail, w345[k - 3]) for k in (3, 4, 5)]
        pairs = [(1, wide, g1), (1, level, m1), (2, both[0][:, 0:256], g2), (2, both[0][:, 256:384], m2)]
        for (k, _, g, m), a in zip(deeper, both[1:]):
            pairs += [(k, a[:, 0:128], g), (k, a[:, 128:256], m)]
        for k, a, out in pairs:
            at = row_of(k) + 1
            for ch in range(CH):
                for t in range(out.shape[1]):
                    out[ch, t, at : at + count, :] += a[count * ch : count * (ch + 1), 128 * t : 128 * (t + 1)]

    def details(counts):
        for g, level, at, out, count in zip((g1, g2, g3, g4, g5), (xs, m1, m2, m3, m4), (8, 1, 1, 1, 1), (d0, d1, d2, d3w, d4w), counts):
            detail(g, level, at, out, count)
        d3[...] = d3w[:, 0, :, 0:64]
        d4[...] = d4w[:, 0, :, 0:32]
        d5[...] = m5[:, 0, 1:5, 0:16]

    for m in (3, 4, 5):
        pl.when(there(-messages[m][2], -messages[m][3]))(copies[m].wait_recv)
    add_rows(rl_in, clm, clp, 2, lambda k: H[k] - 1)
    for k, g in enumerate((g1, g2, g3, g4, g5), 1):
        g[:, :, H[k] + 1 : H[k] + 2, :] = g[:, :, pl.ds(jnp.where(last, H[k], H[k] + 1), 1), :]
    details(H[1:6])
    for m in range(3):
        pl.when(there(-messages[m][2], -messages[m][3]))(copies[m].wait_recv)
    ri[...] = jnp.zeros_like(ri)
    add_rows(rh_in, chm, chp, 3, lambda k: -1)
    details((4,) * 5)
    for copy, (_, _, dr, dc) in zip(copies, messages):
        pl.when(there(dr, dc))(copy.wait_send)


def result_kernel(d0, d1, d2, d3, d4, d5, o0, o1, o2, o3, o4, o5, sem):
    pairs = [(d0.at[:, t], o0.at[:, :, pl.ds(128 * t, 128)]) for t in range(4)]
    pairs += [(d1.at[:, t], o1.at[:, :, pl.ds(128 * t, 128)]) for t in range(2)]
    pairs += [(d2.at[:, 0], o2), (d3, o3), (d4, o4), (d5, o5)]
    copies = [pltpu.make_async_copy(src, dst, sem.at[i]) for i, (src, dst) in enumerate(pairs)]
    for copy in copies:
        copy.start()
    for copy in copies:
        copy.wait()


def body(orthophoto):
    def vmem(*shape, dtype=F32):
        return pltpu.VMEM(shape, dtype)

    held = [(CH, 4, H[0], 128), (CH, 2, H[1], 128), (CH, 1, H[2], 128)]
    held += [(CH, H[3], W[3]), (CH, H[4], W[4]), (CH, H[5], W[5])]
    scratch = [vmem(CH, 4, H[k] + 32, 128) for k in range(6)]
    scratch += [vmem(512, 1024, dtype=BF16), vmem(384, 512, dtype=BF16), vmem(128, 256, dtype=BF16)]
    scratch += [vmem(256, 384, dtype=BF16), vmem(3, 256, 256, dtype=BF16), vmem(128, 1664, dtype=BF16)]
    scratch += [vmem(4, 80, 128), vmem(16, 640), vmem(16, 128)]
    scratch += [vmem(CH, 4, 640), vmem(CH, 2, 640), vmem(8, 512)]
    scratch += [vmem(CH, 4, 640), vmem(CH, 2, 640), vmem(8, 512), vmem(8, 512)]
    scratch += [vmem(CH, 4, 128), vmem(CH, 4, 128), vmem(CH, 2, 128), vmem(CH, 2, 128)]
    scratch += [vmem(CH, t, R[k], 128) for k, t in ((1, 4), (2, 2), (3, 1), (4, 1), (5, 1))]
    scratch += [vmem(CH, t, R[k], 128) for k, t in ((1, 2), (2, 1), (3, 1), (4, 1), (5, 1))]
    scratch += [vmem(CH, 1, H[3], 128), vmem(CH, 1, H[4], 128)]
    scratch += [pltpu.SemaphoreType.DMA((n,)) for n in (12, 8, 8)]
    far = pl.BlockSpec(memory_space=pltpu.HBM)
    inside = pl.BlockSpec(memory_space=pltpu.VMEM)
    inputs = [pltpu.with_memory_space_constraint(jnp.asarray(a), pltpu.HBM) for a in (orthophoto, *tables())]
    arrays = pl.pallas_call(
        exchange_kernel,
        out_shape=[jax.ShapeDtypeStruct(shape, F32) for shape in held],
        in_specs=[far] * len(inputs),
        out_specs=[inside] * len(held),
        scratch_shapes=scratch,
        compiler_params=pltpu.CompilerParams(collective_id=0, has_side_effects=True, vmem_limit_bytes=24 << 20),
    )(*inputs)
    results = pl.pallas_call(
        result_kernel,
        out_shape=[jax.ShapeDtypeStruct((CH, H[k], W[k]), F32) for k in range(6)],
        in_specs=[inside] * len(held),
        out_specs=[far] * 6,
        scratch_shapes=[pltpu.SemaphoreType.DMA((10,))],
        compiler_params=pltpu.CompilerParams(vmem_limit_bytes=8 << 20),
    )(*arrays)
    return tuple(results)


def solution(mesh):
    placed = P(None, "rows", "cols")
    return jax.shard_map(body, mesh=mesh, in_specs=(placed,), out_specs=(placed,) * 6, check_vma=False)
```

time: 15.3 us -> 13.8 us (0.902)
  Pallas kernels: 14.5 us -> 13.1 us
    pallas_call x1, Pallas kernels: 13.2 us -> 12 us  [body(): pl.pallas_call(exchange_kernel, out_shape=[jax.ShapeDtypeStruct(shape, F3...]
    pallas_call x1, Pallas kernels: 1.29 us -> 1.04 us  [body(): pl.pallas_call(result_kernel, out_shape=[jax.ShapeDtypeStruct((CH, H[k],...]
where the time goes in v2:
time: 13.8 us; the launch traced here: 13.7 us
  Pallas kernels  13.1 us (95%)
  between operations  0.64 us (5%)
    pallas_call x1, Pallas kernels, body(): pl.pallas_call(exchange_kernel, out_shape=[jax.ShapeDtypeStruct(shape, F3...  12 us
    pallas_call x1, Pallas kernels, body(): pl.pallas_call(result_kernel, out_shape=[jax.ShapeDtypeStruct((CH, H[k],...  1.04 us

profile of v2, /device:TPU:25, one launch (start us, length us, event | category | flops | bytes accessed | tf_op | source)
XLA Modules:
  0.0 13.7 jit_solution(9914006328957232590)
XLA Ops:
  0.6 12.0 %shard_map.136 = (f32[3,4,128,128]{3,2,1,0:T(8,128)S(1)}, f32[3,2,64,128]{3,2,1,0:T(8,128)S(1)}, f32[3,1,32,128]{3,2,1,0:T(8,128)S(1)}, f32[3,16,64]{2,1,0:T(8,1...) custom-call(f32[3,128,512]{2,1,0:T(8,128)} %x_hbm.1, bf16[2,128,1024]{2,1,0:T(8,128)(2,1)} %constant.16.clone.tlow_hbm, ...), custom_call_target="tpu_custom_call" | custom-call | tf_op jit(solution)/shard_map/pallas_call | solution.py:434
  12.6 1.0 %shard_map.137 = (f32[3,128,512]{2,1,0:T(8,128)}, f32[3,64,256]{2,1,0:T(8,128)}, f32[3,32,128]{2,1,0:T(8,128)}, f32[3,16,64]{2,1,0:T(8,128)}, f32[3,8,32]{2,1,0:T(8,128)}, /*index=5*/f32[3,4,16]{2,1,0:T(4,128)}) custom-call(f32[3,4,128,128]{3,2,1,0:T(8,128)S(1)} %get-tuple-element.12.d0, f32[3,2,64,128]{3,2,1,0:T(8,128)S(1)} %get-tuple-element.13.d1, ...), custom_call_target="tpu_custom_call" | custom-call | tf_op jit(solution)/shard_map/pallas_call | solution.py:442

commit v3 on v2

--- a/solution.py
+++ b/solution.py
@@ -146,10 +146,14 @@
     h = H[k]
     count = R[k]
 
-    def tap(o):
-        return src[:, t, pl.ds(6 + o, count, stride=2), :]
-
-    dst[:, t, 7 : 7 + count, :] = (tap(-2) + tap(2)) + (tap(-1) + tap(1)) * 4.0 + tap(0) * 6.0
+    def tap(ch, at, o):
+        return src[ch, t, pl.ds(6 + 2 * at + o, 8, stride=2), :]
+
+    for ch in range(CH):
+        for at in range(0, count, 8):
+            dst[ch, t, 7 + at : 15 + at, :] = (
+                (tap(ch, at, -2) + tap(ch, at, 2)) + (tap(ch, at, -1) + tap(ch, at, 1)) * 4.0 + tap(ch, at, 0) * 6.0
+            )
     mirror(dst, t, h, first, last, k < LEVELS)
 
 
@@ -202,7 +206,7 @@
         pltpu.make_async_copy(w345_hbm, w345, load_sem.at[10]),
         pltpu.make_async_copy(arrive_hbm, arrive, load_sem.at[11]),
     ]
-    for copy in loads:
+    for copy in loads[:7]:
         copy.start()
 
     def there(dr, dc):
@@ -244,10 +248,12 @@
     ci[...] = jnp.zeros_like(ci)
     rh[...] = jnp.zeros_like(rh)
 
+    for copy in loads[:7]:
+        copy.wait()
     for t in range(4):
-        loads[t].wait()
         mirror(xs, t, ROWS, first, last, True)
-        for k in range(1, LEVELS + 1):
+    for k in range(1, LEVELS + 1):
+        for t in range(4):
             reduce_rows(k, t, ys[k - 1], ys[k], first, last)
 
     for k in range(1, LEVELS + 1):
@@ -256,8 +262,6 @@
             srs[:, at : at + 3, :] = ys[k][ch, :, 7 + H[k] : 10 + H[k], :]
             at = 16 * (k - 1) + 9 + 2 * ch
             srs[:, at : at + 2, :] = ys[k][ch, :, 7:9, :]
-    for copy in loads[4:7]:
-        copy.wait()
     strips = jnp.concatenate([srs[t] for t in range(4)], axis=1)
     near = dot3(strips[0:32], tv[:, 0:512])
     deep = dot3(strips[32:80], tv[:, 512:1024])
@@ -286,6 +290,9 @@
         )
         if m < 6:
             pl.when(there(dr, dc))(copies[m].start)
+
+    for copy in loads[7:]:
+        copy.start()
 
     outer = jnp.concatenate([rows_of(k, ys[k], (0, 3)) for k in range(1, LEVELS + 1)], axis=0)
     table = jnp.concatenate([tv[0:128], tv[384:512]], axis=0)

time: 13.8 us -> 14.2 us (1.029)
  Pallas kernels: 13.1 us -> 13.4 us
    pallas_call x1, Pallas kernels: 12 us -> 12.3 us  [body(): pl.pallas_call(exchange_kernel, out_shape=[jax.ShapeDtypeStruct(shape, F3...]
where the time goes in v3:
time: 14.2 us; the launch traced here: 14 us
  Pallas kernels  13.4 us (94%)
  between operations  0.64 us (5%)
    pallas_call x1, Pallas kernels, body(): pl.pallas_call(exchange_kernel, out_shape=[jax.ShapeDtypeStruct(shape, F3...  12.3 us
    pallas_call x1, Pallas kernels, body(): pl.pallas_call(result_kernel, out_shape=[jax.ShapeDtypeStruct((CH, H[k],...  1.04 us

profile of v3, /device:TPU:25, one launch (start us, length us, event | category | flops | bytes accessed | tf_op | source)
XLA Modules:
  0.0 14.0 jit_solution(7894657130642072469)
XLA Ops:
  0.6 12.3 %shard_map.136 = (f32[3,4,128,128]{3,2,1,0:T(8,128)S(1)}, f32[3,2,64,128]{3,2,1,0:T(8,128)S(1)}, f32[3,1,32,128]{3,2,1,0:T(8,128)S(1)}, f32[3,16,64]{2,1,0:T(8,1...) custom-call(f32[3,128,512]{2,1,0:T(8,128)} %x_hbm.1, bf16[2,128,1024]{2,1,0:T(8,128)(2,1)} %constant.16.clone.tlow_hbm, ...), custom_call_target="tpu_custom_call" | custom-call | tf_op jit(solution)/shard_map/pallas_call | solution.py:441
  13.0 1.0 %shard_map.137 = (f32[3,128,512]{2,1,0:T(8,128)}, f32[3,64,256]{2,1,0:T(8,128)}, f32[3,32,128]{2,1,0:T(8,128)}, f32[3,16,64]{2,1,0:T(8,128)}, f32[3,8,32]{2,1,0:T(8,128)}, /*index=5*/f32[3,4,16]{2,1,0:T(4,128)}) custom-call(f32[3,4,128,128]{3,2,1,0:T(8,128)S(1)} %get-tuple-element.12.d0, f32[3,2,64,128]{3,2,1,0:T(8,128)S(1)} %get-tuple-element.13.d1, ...), custom_call_target="tpu_custom_call" | custom-call | tf_op jit(solution)/shard_map/pallas_call | solution.py:449

commit v4 on v3

--- a/solution.py
+++ b/solution.py
@@ -46,19 +46,21 @@
 def reduction_table(low, high):
     t = column_reductions(low, high)
 
-    def edge(k):
-        cells = (W[k] - 1, W[k] - 1 if high else W[k], W[k] + 1, 1 if low else -1, 0)
-        return t[k][:, [c + 1 for c in cells]]
+    def fill(a, at, k):
+        beyond, before = W[k] - 1 if high else W[k], 1 if low else -1
+        cells = (W[k] - 1, beyond, W[k] + 1, before, 0)
+        a[:, at + 8 * (k - 1) : at + 8 * (k - 1) + 5] = t[k][:, [c + 1 for c in cells]]
+        a[:, at + 112 + 2 * (k - 1) : at + 114 + 2 * (k - 1)] = t[k][:, [beyond + 1, before + 1]]
 
     first = np.zeros((COLS, 512))
     first[:, 0:256] = t[1][:, 1:257]
     first[:, 384:512] = t[2][:, 1:129]
     last = np.zeros((COLS, 256))
     for k in (3, 4, 5):
-        last[:, 8 * (k - 1) : 8 * (k - 1) + 5] = edge(k)
+        fill(last, 0, k)
         last[:, 128 + POS[k] : 128 + POS[k] + W[k]] = t[k][:, 1 : W[k] + 1]
     for k in (1, 2):
-        first[:, 256 + 8 * (k - 1) : 256 + 8 * (k - 1) + 5] = edge(k)
+        fill(first, 256, k)
     top = np.asarray(last.astype(jnp.bfloat16), np.float64)
     rest = np.asarray((last - top).astype(jnp.bfloat16), np.float64)
     assert np.array_equal(top + rest, last)
@@ -81,10 +83,10 @@
     for c in range(W[k]):
         spread[main_at + c] = expansion_row(k, c)
         keep[main_at + c, c] = 1
-    own = edge_at + 8 * (k - 1)
-    came = own + 64
-    spread[own + 1] = expansion_row(k, W[k])
-    spread[own + 3] = expansion_row(k, -1)
+    own = edge_at + 112 + 2 * (k - 1)
+    came = edge_at + 64 + 8 * (k - 1)
+    spread[own] = expansion_row(k, W[k])
+    spread[own + 1] = expansion_row(k, -1)
     for s, cell in enumerate((-1, 0, 1, W[k] - 1, W[k])):
         spread[came + s] = expansion_row(k, cell)
         if 0 <= cell < W[k]:
@@ -180,8 +182,8 @@
 def exchange_kernel(
     x_hbm, tlow_hbm, tmid_hbm, thigh_hbm, v1_hbm, s1_hbm, w2_hbm, w345_hbm, arrive_hbm,
     d0, d1, d2, d3, d4, d5,
-    xs, y1, y2, y3, y4, y5, tv, v1, s1, w2, w345, arrive, srs, ri, ci,
-    rh, rl, cb, rh_in, rl_in, cbm, cbp, chm, chp, clm, clp,
+    xs, y1, y2, y3, y4, y5, tv, v1, s1, w2, w345, arrive, srs, ci,
+    rh, rl, kh, kl, cb, rh_in, rl_in, cbm, cbp, chm, chp, clm, clp,
     g1, g2, g3, g4, g5, m1, m2, m3, m4, m5, d3w, d4w,
     load_sem, send_sem, recv_sem,
 ):
@@ -217,14 +219,13 @@
             ok = jnp.logical_and(ok, west if dc < 0 else east)
         return ok
 
-    edge = pl.ds(256, 128)
     messages = [
         (rh, rh_in, 1, 0),
-        (rh.at[:, :, edge], chm, 1, 1),
-        (rh.at[:, :, edge], chp, 1, -1),
+        (kh, chm, 1, 1),
+        (kh, chp, 1, -1),
         (rl, rl_in, -1, 0),
-        (rl.at[:, :, edge], clm, -1, 1),
-        (rl.at[:, :, edge], clp, -1, -1),
+        (kl, clm, -1, 1),
+        (kl, clp, -1, -1),
         (cb, cbm, 0, 1),
         (cb, cbp, 0, -1),
     ]
@@ -244,11 +245,11 @@
         ys[k][:, :, 0:8, :] = jnp.zeros((CH, 4, 8, 128), F32)
         ys[k][:, :, 8 + H[k] : 32 + H[k], :] = jnp.zeros((CH, 4, 24, 128), F32)
     srs[...] = jnp.zeros_like(srs)
-    ri[...] = jnp.zeros_like(ri)
     ci[...] = jnp.zeros_like(ci)
-    rh[...] = jnp.zeros_like(rh)
-
-    for copy in loads[:7]:
+    for a in (rh, kh, kl):
+        a[...] = jnp.zeros_like(a)
+
+    for copy in loads[:4]:
         copy.wait()
     for t in range(4):
         mirror(xs, t, ROWS, first, last, True)
@@ -262,6 +263,8 @@
             srs[:, at : at + 3, :] = ys[k][ch, :, 7 + H[k] : 10 + H[k], :]
             at = 16 * (k - 1) + 9 + 2 * ch
             srs[:, at : at + 2, :] = ys[k][ch, :, 7:9, :]
+    for copy in loads[4:7]:
+        copy.wait()
     strips = jnp.concatenate([srs[t] for t in range(4)], axis=1)
     near = dot3(strips[0:32], tv[:, 0:512])
     deep = dot3(strips[32:80], tv[:, 512:1024])
@@ -270,11 +273,16 @@
     cells = jnp.where(lane < 32, deep[16:32, 0:128], deep[32:48, 0:128])
     cells = jnp.where(lane < 24, deep[0:16, 0:128], cells)
     cells = jnp.where(lane < 8, near[0:16, 256:384], jnp.where(lane < 16, near[16:32, 256:384], cells))
+    beside = jnp.where(lane < 118, deep[0:16, 0:128], jnp.where(lane < 120, deep[16:32, 0:128], deep[32:48, 0:128]))
+    beside = jnp.where(lane < 114, near[0:16, 256:384], jnp.where(lane < 116, near[16:32, 256:384], beside))
     small = jnp.where(lane < 64, deep[0:16, 128:256], jnp.where(lane < 96, deep[16:32, 128:256], deep[32:48, 128:256]))
-    strips = jnp.concatenate([near[0:16, 0:256], cells, near[16:32, 384:512], small], axis=1)
-    for ch in range(CH):
-        rh[ch, 0:3, :] = strips[3 * ch : 3 * ch + 3]
-        rl[ch, :, :] = strips[9 + 2 * ch : 11 + 2 * ch]
+    small = jnp.where(lane < 112, small, beside)
+    for t, a in enumerate((near[0:16, 0:128], near[0:16, 128:256], near[16:32, 384:512], small)):
+        rh[pl.ds(t, 9, stride=4), :] = a[0:9]
+        rl[pl.ds(t, 6, stride=4), :] = a[9:15]
+    ci[...] = jnp.where(lane < 40, cells, 0.0)
+    kh[0:3, :] = sum(pltpu.roll(ci[pl.ds(i, CH, stride=3), :], 40 * i, 1) for i in range(3))
+    kl[0:3, :] = sum(pltpu.roll(ci[pl.ds(9 + i, CH, stride=2), :], 40 * i, 1) for i in range(2))
 
     neighbours = (up.astype(jnp.int32) + down.astype(jnp.int32) + 1) * (
         west.astype(jnp.int32) + east.astype(jnp.int32) + 1
@@ -363,18 +371,22 @@
         add(k, more, g, (0,))
         add(k, more, m, (0,), 1)
 
-    side = jnp.bitwise_and(lax.broadcasted_iota(jnp.int32, (1, 128), 1), 7) < 3
+    side = jnp.bitwise_and(lane, 7) < 3
+    middle = jnp.logical_and(lane >= 64, lane < 104)
+    ci[...] = jnp.zeros_like(ci)
 
     def add_rows(strip, minus, plus, count, row_of):
-        for ch in range(CH):
-            ri[count * ch : count * (ch + 1), :] = strip[ch, 0:count, :]
-            ci[count * ch : count * (ch + 1), :] = jnp.where(side, minus[ch, 0:count, :], plus[ch, 0:count, :])
-        strips = ri[...]
-        cells = strips[:, 256:384] + pltpu.roll(ci[...], 64, 1)
-        wide = dot3(jnp.concatenate([strips[:, 0:256], cells], axis=1), v1[...])
-        level = strips[:, 0:256] + dot3(cells, s1[...])
-        both = [dot3(jnp.concatenate([cells, strips[:, 384:512]], axis=1), w2[...])]
-        tail = jnp.concatenate([cells, strips[:, 512:640]], axis=1)
+        corner = jnp.where(side[0:4], minus[...], plus[...])
+        for i in range(count):
+            ci[pl.ds(i, CH, stride=count), :] = pltpu.roll(corner, (64 - 40 * i) % 128, 1)[0:CH]
+        rows = CH * count
+        fill = jnp.zeros((16 - rows, 128), F32)
+        tiles = [jnp.concatenate([strip[pl.ds(t, rows, stride=4), :], fill], axis=0) for t in range(4)]
+        cells = jnp.where(lane < 112, jnp.where(middle, ci[...], 0.0), tiles[3])
+        wide = dot3(jnp.concatenate([tiles[0], tiles[1], cells], axis=1), v1[...])
+        level = jnp.concatenate(tiles[0:2], axis=1) + dot3(cells, s1[...])
+        both = [dot3(jnp.concatenate([cells, tiles[2]], axis=1), w2[...])]
+        tail = jnp.concatenate([cells, tiles[3]], axis=1)
         both += [dot3(tail, w345[k - 3]) for k in (3, 4, 5)]
         pairs = [(1, wide, g1), (1, level, m1), (2, both[0][:, 0:256], g2), (2, both[0][:, 256:384], m2)]
         for (k, _, g, m), a in zip(deeper, both[1:]):
@@ -400,7 +412,6 @@
     details(H[1:6])
     for m in range(3):
         pl.when(there(-messages[m][2], -messages[m][3]))(copies[m].wait_recv)
-    ri[...] = jnp.zeros_like(ri)
     add_rows(rh_in, chm, chp, 3, lambda k: -1)
     details((4,) * 5)
     for copy, (_, _, dr, dc) in zip(copies, messages):
@@ -427,10 +438,10 @@
     scratch = [vmem(CH, 4, H[k] + 32, 128) for k in range(6)]
     scratch += [vmem(512, 1024, dtype=BF16), vmem(384, 512, dtype=BF16), vmem(128, 256, dtype=BF16)]
     scratch += [vmem(256, 384, dtype=BF16), vmem(3, 256, 256, dtype=BF16), vmem(128, 1664, dtype=BF16)]
-    scratch += [vmem(4, 80, 128), vmem(16, 640), vmem(16, 128)]
-    scratch += [vmem(CH, 4, 640), vmem(CH, 2, 640), vmem(8, 512)]
-    scratch += [vmem(CH, 4, 640), vmem(CH, 2, 640), vmem(8, 512), vmem(8, 512)]
-    scratch += [vmem(CH, 4, 128), vmem(CH, 4, 128), vmem(CH, 2, 128), vmem(CH, 2, 128)]
+    scratch += [vmem(4, 80, 128), vmem(16, 128)]
+    scratch += [vmem(40, 128), vmem(24, 128), vmem(4, 128), vmem(4, 128), vmem(8, 512)]
+    scratch += [vmem(40, 128), vmem(24, 128), vmem(8, 512), vmem(8, 512)]
+    scratch += [vmem(4, 128)] * 4
     scratch += [vmem(CH, t, R[k], 128) for k, t in ((1, 4), (2, 2), (3, 1), (4, 1), (5, 1))]
     scratch += [vmem(CH, t, R[k], 128) for k, t in ((1, 2), (2, 1), (3, 1), (4, 1), (5, 1))]
     scratch += [vmem(CH, 1, H[3], 128), vmem(CH, 1, H[4], 128)]

time: 14.2 us -> 13.8 us (0.972)
  Pallas kernels: 13.4 us -> 13 us
    pallas_call x1, Pallas kernels: 12.3 us -> 11.9 us  [body(): pl.pallas_call(exchange_kernel, out_shape=[jax.ShapeDtypeStruct(shape, F3...]
where the time goes in v4:
time: 13.8 us; the launch traced here: 13.6 us
  Pallas kernels  13 us (94%)
  between operations  0.64 us (5%)
    pallas_call x1, Pallas kernels, body(): pl.pallas_call(exchange_kernel, out_shape=[jax.ShapeDtypeStruct(shape, F3...  11.9 us
    pallas_call x1, Pallas kernels, body(): pl.pallas_call(result_kernel, out_shape=[jax.ShapeDtypeStruct((CH, H[k],...  1.04 us

profile of v4, /device:TPU:25, one launch (start us, length us, event | category | flops | bytes accessed | tf_op | source)
XLA Modules:
  0.0 13.6 jit_solution(5537886677729249739)
XLA Ops:
  0.6 11.9 %shard_map.136 = (f32[3,4,128,128]{3,2,1,0:T(8,128)S(1)}, f32[3,2,64,128]{3,2,1,0:T(8,128)S(1)}, f32[3,1,32,128]{3,2,1,0:T(8,128)S(1)}, f32[3,16,64]{2,1,0:T(8,1...) custom-call(f32[3,128,512]{2,1,0:T(8,128)} %x_hbm.1, bf16[2,128,1024]{2,1,0:T(8,128)(2,1)} %constant.16.clone.tlow_hbm, ...), custom_call_target="tpu_custom_call" | custom-call | tf_op jit(solution)/shard_map/pallas_call | solution.py:452
  12.6 1.0 %shard_map.137 = (f32[3,128,512]{2,1,0:T(8,128)}, f32[3,64,256]{2,1,0:T(8,128)}, f32[3,32,128]{2,1,0:T(8,128)}, f32[3,16,64]{2,1,0:T(8,128)}, f32[3,8,32]{2,1,0:T(8,128)}, /*index=5*/f32[3,4,16]{2,1,0:T(4,128)}) custom-call(f32[3,4,128,128]{3,2,1,0:T(8,128)S(1)} %get-tuple-element.12.d0, f32[3,2,64,128]{3,2,1,0:T(8,128)S(1)} %get-tuple-element.13.d1, ...), custom_call_target="tpu_custom_call" | custom-call | tf_op jit(solution)/shard_map/pallas_call | solution.py:460

commit v5 on v4

--- a/solution.py
+++ b/solution.py
@@ -144,25 +144,28 @@
     return p[0:m] + p[m : 2 * m] + p[2 * m : 3 * m]
 
 
-def reduce_rows(k, t, src, dst, first, last):
-    h = H[k]
-    count = R[k]
-
-    def tap(ch, at, o):
-        return src[ch, t, pl.ds(6 + 2 * at + o, 8, stride=2), :]
-
+BELOW = [None, (18, 26, 34, 42, 50, 58), (10, 18, 26), (6, 14), (4,), (3,)]
+ABOVE = [None, (-1, 7, 15), (-1, 7), (-1,), (-1,), (-1,)]
+
+
+def reduce_rows(t, src, dst, starts):
     for ch in range(CH):
-        for at in range(0, count, 8):
-            dst[ch, t, 7 + at : 15 + at, :] = (
-                (tap(ch, at, -2) + tap(ch, at, 2)) + (tap(ch, at, -1) + tap(ch, at, 1)) * 4.0 + tap(ch, at, 0) * 6.0
-            )
-    mirror(dst, t, h, first, last, k < LEVELS)
-
-
-def mirror(a, t, h, first, last, outer):
-    a[:, t, 7:8, :] = a[:, t, pl.ds(jnp.where(first, 9, 7), 1), :]
-    if outer:
+        for j in starts:
+
+            def tap(o):
+                return src[ch, t, pl.ds(8 + 2 * j + o, 8, stride=2), :]
+
+            dst[ch, t, 8 + j : 16 + j, :] = (tap(-2) + tap(2)) + (tap(-1) + tap(1)) * 4.0 + tap(0) * 6.0
+
+
+def mirror_start(a, first):
+    for t in range(4):
+        a[:, t, 7:8, :] = a[:, t, pl.ds(jnp.where(first, 9, 7), 1), :]
         a[:, t, 6:7, :] = a[:, t, pl.ds(jnp.where(first, 10, 6), 1), :]
+
+
+def mirror_end(a, h, last):
+    for t in range(4):
         a[:, t, 8 + h : 9 + h, :] = a[:, t, pl.ds(jnp.where(last, 6 + h, 8 + h), 1), :]
 
 
@@ -251,39 +254,35 @@
 
     for copy in loads[:4]:
         copy.wait()
-    for t in range(4):
-        mirror(xs, t, ROWS, first, last, True)
     for k in range(1, LEVELS + 1):
+        mirror_end(ys[k - 1], H[k - 1], last)
         for t in range(4):
-            reduce_rows(k, t, ys[k - 1], ys[k], first, last)
-
-    for k in range(1, LEVELS + 1):
+            reduce_rows(t, ys[k - 1], ys[k], BELOW[k])
         for ch in range(CH):
             at = 16 * (k - 1) + 3 * ch
             srs[:, at : at + 3, :] = ys[k][ch, :, 7 + H[k] : 10 + H[k], :]
-            at = 16 * (k - 1) + 9 + 2 * ch
-            srs[:, at : at + 2, :] = ys[k][ch, :, 7:9, :]
     for copy in loads[4:7]:
         copy.wait()
-    strips = jnp.concatenate([srs[t] for t in range(4)], axis=1)
-    near = dot3(strips[0:32], tv[:, 0:512])
-    deep = dot3(strips[32:80], tv[:, 512:1024])
-    deep = deep[:, 0:256] + deep[:, 256:512]
     lane = lax.broadcasted_iota(jnp.int32, (16, 128), 1)
-    cells = jnp.where(lane < 32, deep[16:32, 0:128], deep[32:48, 0:128])
-    cells = jnp.where(lane < 24, deep[0:16, 0:128], cells)
-    cells = jnp.where(lane < 8, near[0:16, 256:384], jnp.where(lane < 16, near[16:32, 256:384], cells))
-    beside = jnp.where(lane < 118, deep[0:16, 0:128], jnp.where(lane < 120, deep[16:32, 0:128], deep[32:48, 0:128]))
-    beside = jnp.where(lane < 114, near[0:16, 256:384], jnp.where(lane < 116, near[16:32, 256:384], beside))
-    small = jnp.where(lane < 64, deep[0:16, 128:256], jnp.where(lane < 96, deep[16:32, 128:256], deep[32:48, 128:256]))
-    small = jnp.where(lane < 112, small, beside)
-    for t, a in enumerate((near[0:16, 0:128], near[0:16, 128:256], near[16:32, 384:512], small)):
-        rh[pl.ds(t, 9, stride=4), :] = a[0:9]
-        rl[pl.ds(t, 6, stride=4), :] = a[9:15]
-    ci[...] = jnp.where(lane < 40, cells, 0.0)
-    kh[0:3, :] = sum(pltpu.roll(ci[pl.ds(i, CH, stride=3), :], 40 * i, 1) for i in range(3))
-    kl[0:3, :] = sum(pltpu.roll(ci[pl.ds(9 + i, CH, stride=2), :], 40 * i, 1) for i in range(2))
-
+
+    def form_strips(out, corners, count):
+        strips = jnp.concatenate([srs[t] for t in range(4)], axis=1)
+        near = dot3(strips[0:32], tv[:, 0:512])
+        deep = dot3(strips[32:80], tv[:, 512:1024])
+        deep = deep[:, 0:256] + deep[:, 256:512]
+        cells = jnp.where(lane < 32, deep[16:32, 0:128], deep[32:48, 0:128])
+        cells = jnp.where(lane < 24, deep[0:16, 0:128], cells)
+        cells = jnp.where(lane < 8, near[0:16, 256:384], jnp.where(lane < 16, near[16:32, 256:384], cells))
+        beside = jnp.where(lane < 118, deep[0:16, 0:128], jnp.where(lane < 120, deep[16:32, 0:128], deep[32:48, 0:128]))
+        beside = jnp.where(lane < 114, near[0:16, 256:384], jnp.where(lane < 116, near[16:32, 256:384], beside))
+        small = jnp.where(lane < 96, deep[16:32, 128:256], deep[32:48, 128:256])
+        small = jnp.where(lane < 64, deep[0:16, 128:256], jnp.where(lane < 112, small, beside))
+        for t, a in enumerate((near[0:16, 0:128], near[0:16, 128:256], near[16:32, 384:512], small)):
+            out[pl.ds(t, CH * count, stride=4), :] = a[0 : CH * count]
+        ci[...] = jnp.where(lane < 40, cells, 0.0)
+        corners[0:3, :] = sum(pltpu.roll(ci[pl.ds(i, CH, stride=count), :], 40 * i, 1) for i in range(count))
+
+    form_strips(rh, kh, 3)
     neighbours = (up.astype(jnp.int32) + down.astype(jnp.int32) + 1) * (
         west.astype(jnp.int32) + east.astype(jnp.int32) + 1
     ) - 1
@@ -296,11 +295,24 @@
                 device_id=(r + dr, c + dc), device_id_type=MESH,
             )
         )
-        if m < 6:
-            pl.when(there(dr, dc))(copies[m].start)
+    for m in (1, 2, 0):
+        pl.when(there(*messages[m][2:]))(copies[m].start)
 
     for copy in loads[7:]:
         copy.start()
+
+    for k in range(1, LEVELS + 1):
+        mirror_start(ys[k - 1], first)
+        for t in range(4):
+            reduce_rows(t, ys[k - 1], ys[k], ABOVE[k])
+    mirror_start(y5, first)
+    for k in range(1, LEVELS + 1):
+        for ch in range(CH):
+            at = 16 * (k - 1) + 2 * ch
+            srs[:, at : at + 2, :] = ys[k][ch, :, 7:9, :]
+    form_strips(rl, kl, 2)
+    for m in (3, 4, 5):
+        pl.when(there(*messages[m][2:]))(copies[m].start)
 
     outer = jnp.concatenate([rows_of(k, ys[k], (0, 3)) for k in range(1, LEVELS + 1)], axis=0)
     table = jnp.concatenate([tv[0:128], tv[384:512]], axis=0)

time: 13.8 us -> 14.2 us (1.029)
  Pallas kernels: 13 us -> 13.4 us
    pallas_call x1, Pallas kernels: 11.9 us -> 12.3 us  [body(): pl.pallas_call(exchange_kernel, out_shape=[jax.ShapeDtypeStruct(shape, F3...]
where the time goes in v5:
time: 14.2 us; the launch traced here: 14 us
  Pallas kernels  13.4 us (94%)
  between operations  0.64 us (5%)
    pallas_call x1, Pallas kernels, body(): pl.pallas_call(exchange_kernel, out_shape=[jax.ShapeDtypeStruct(shape, F3...  12.3 us
    pallas_call x1, Pallas kernels, body(): pl.pallas_call(result_kernel, out_shape=[jax.ShapeDtypeStruct((CH, H[k],...  1.04 us

profile of v5, /device:TPU:25, one launch (start us, length us, event | category | flops | bytes accessed | tf_op | source)
XLA Modules:
  0.0 14.0 jit_solution(2004177842984624377)
XLA Ops:
  0.6 12.3 %shard_map.136 = (f32[3,4,128,128]{3,2,1,0:T(8,128)S(1)}, f32[3,2,64,128]{3,2,1,0:T(8,128)S(1)}, f32[3,1,32,128]{3,2,1,0:T(8,128)S(1)}, f32[3,16,64]{2,1,0:T(8,1...) custom-call(f32[3,128,512]{2,1,0:T(8,128)} %x_hbm.1, bf16[2,128,1024]{2,1,0:T(8,128)(2,1)} %constant.16.clone.tlow_hbm, ...), custom_call_target="tpu_custom_call" | custom-call | tf_op jit(solution)/shard_map/pallas_call | solution.py:464
  13.0 1.0 %shard_map.137 = (f32[3,128,512]{2,1,0:T(8,128)}, f32[3,64,256]{2,1,0:T(8,128)}, f32[3,32,128]{2,1,0:T(8,128)}, f32[3,16,64]{2,1,0:T(8,128)}, f32[3,8,32]{2,1,0:T(8,128)}, /*index=5*/f32[3,4,16]{2,1,0:T(4,128)}) custom-call(f32[3,4,128,128]{3,2,1,0:T(8,128)S(1)} %get-tuple-element.12.d0, f32[3,2,64,128]{3,2,1,0:T(8,128)S(1)} %get-tuple-element.13.d1, ...), custom_call_target="tpu_custom_call" | custom-call | tf_op jit(solution)/shard_map/pallas_call | solution.py:472

commit v6 on v5

--- a/solution.py
+++ b/solution.py
@@ -283,6 +283,64 @@
         corners[0:3, :] = sum(pltpu.roll(ci[pl.ds(i, CH, stride=count), :], 40 * i, 1) for i in range(count))
 
     form_strips(rh, kh, 3)
+    place = lax.broadcasted_iota(jnp.int32, (8, 512), 1)
+
+    def of_level(k, a):
+        ok = place < (BASE[k + 1] if k < LEVELS else 480)
+        return jnp.where(jnp.logical_and(ok, place >= BASE[k]), a, 0.0)
+
+    def put(k, a, out):
+        for ch in range(CH):
+            for t in range(out.shape[1]):
+                out[ch, t] = a[R[k] * ch : R[k] * (ch + 1), 128 * t : 128 * (t + 1)]
+
+    deeper = ((3, 0, g3, m3), (4, 72, g4, m4), (5, 112, g5, m5))
+
+    def reduce_rest():
+        for k in range(1, LEVELS + 1):
+            mirror_start(ys[k - 1], first)
+            for t in range(4):
+                reduce_rows(t, ys[k - 1], ys[k], ABOVE[k])
+        mirror_start(y5, first)
+        for k in range(1, LEVELS + 1):
+            for ch in range(CH):
+                at = 16 * (k - 1) + 2 * ch
+                srs[:, at : at + 2, :] = ys[k][ch, :, 7:9, :]
+        form_strips(rl, kl, 2)
+        outer = jnp.concatenate([rows_of(k, ys[k], (0, 3)) for k in range(1, LEVELS + 1)], axis=0)
+        table = jnp.concatenate([tv[0:128], tv[384:512]], axis=0)
+        turned = dot3(outer, jnp.concatenate([table[:, 256:384], table[:, 768:896]], axis=1))
+        turned = jnp.concatenate([turned[:, 0:128] + turned[:, 128:256], jnp.zeros((32, 128), F32)], axis=0)
+        turned = jnp.transpose(turned)
+        cb[...] = sum(of_level(k, turned[8 * (k - 1) : 8 * k]) for k in range(1, LEVELS + 1))
+
+    def expand_own():
+        for copy in loads[7:]:
+            copy.start()
+        p12 = dot3(jnp.concatenate([rows_of(k, ys[k], range(4)) for k in (1, 2)], axis=0), tv[:, 0:512])
+        p345 = dot3(jnp.concatenate([rows_of(k, ys[k], range(4)) for k in (3, 4, 5)], axis=0), tv[:, 512:1024])
+        p345 = p345[:, 0:256] + p345[:, 256:512]
+
+        for copy in loads[7:]:
+            copy.wait()
+        put(1, dot3(p12[0:224, 0:384], v1[...]), g1)
+        put(1, p12, m1)
+        both = dot3(p12[208:336, 256:512], w2[...])
+        put(2, both[8:, 0:256], g2)
+        put(2, both[8:, 256:384], m2)
+        for k, at, g, m in deeper:
+            both = dot3(p345[at : at + 16 * -(-3 * R[k] // 16)], w345[k - 3])
+            skip = BASE[k] - BASE[3] - at
+            put(k, both[skip:, 0:128], g)
+            put(k, both[skip:, 128:256], m)
+
+    early = lax.rem(r, 8) == 0
+
+    @pl.when(early)
+    def _():
+        reduce_rest()
+        expand_own()
+
     neighbours = (up.astype(jnp.int32) + down.astype(jnp.int32) + 1) * (
         west.astype(jnp.int32) + east.astype(jnp.int32) + 1
     ) - 1
@@ -298,90 +356,20 @@
     for m in (1, 2, 0):
         pl.when(there(*messages[m][2:]))(copies[m].start)
 
-    for copy in loads[7:]:
-        copy.start()
-
-    for k in range(1, LEVELS + 1):
-        mirror_start(ys[k - 1], first)
-        for t in range(4):
-            reduce_rows(t, ys[k - 1], ys[k], ABOVE[k])
-    mirror_start(y5, first)
-    for k in range(1, LEVELS + 1):
-        for ch in range(CH):
-            at = 16 * (k - 1) + 2 * ch
-            srs[:, at : at + 2, :] = ys[k][ch, :, 7:9, :]
-    form_strips(rl, kl, 2)
-    for m in (3, 4, 5):
+
+    @pl.when(jnp.logical_not(early))
+    def _():
+        reduce_rest()
+
+    for m in range(3, 8):
         pl.when(there(*messages[m][2:]))(copies[m].start)
-
-    outer = jnp.concatenate([rows_of(k, ys[k], (0, 3)) for k in range(1, LEVELS + 1)], axis=0)
-    table = jnp.concatenate([tv[0:128], tv[384:512]], axis=0)
-    turned = dot3(outer, jnp.concatenate([table[:, 256:384], table[:, 768:896]], axis=1))
-    turned = jnp.concatenate([turned[:, 0:128] + turned[:, 128:256], jnp.zeros((32, 128), F32)], axis=0)
-    turned = jnp.transpose(turned)
-    place = lax.broadcasted_iota(jnp.int32, (8, 512), 1)
-
-    def of_level(k, a):
-        ok = place < (BASE[k + 1] if k < LEVELS else 480)
-        return jnp.where(jnp.logical_and(ok, place >= BASE[k]), a, 0.0)
-
-    cb[...] = sum(of_level(k, turned[8 * (k - 1) : 8 * k]) for k in range(1, LEVELS + 1))
-    for m in (6, 7):
-        pl.when(there(*messages[m][2:]))(copies[m].start)
-
-    for copy in loads[7:]:
-        copy.wait()
-    p12 = dot3(jnp.concatenate([rows_of(k, ys[k], range(4)) for k in (1, 2)], axis=0), tv[:, 0:512])
-    p345 = dot3(jnp.concatenate([rows_of(k, ys[k], range(4)) for k in (3, 4, 5)], axis=0), tv[:, 512:1024])
-    p345 = p345[:, 0:256] + p345[:, 256:512]
-
-    def put(k, a, out):
-        for ch in range(CH):
-            for t in range(out.shape[1]):
-                out[ch, t] = a[R[k] * ch : R[k] * (ch + 1), 128 * t : 128 * (t + 1)]
-
-    put(1, dot3(p12[0:224, 0:384], v1[...]), g1)
-    put(1, p12, m1)
-    both = dot3(p12[208:336, 256:512], w2[...])
-    put(2, both[8:, 0:256], g2)
-    put(2, both[8:, 256:384], m2)
-    deeper = ((3, 0, g3, m3), (4, 72, g4, m4), (5, 112, g5, m5))
-    for k, at, g, m in deeper:
-        both = dot3(p345[at : at + 16 * -(-3 * R[k] // 16)], w345[k - 3])
-        skip = BASE[k] - BASE[3] - at
-        put(k, both[skip:, 0:128], g)
-        put(k, both[skip:, 128:256], m)
+    pl.when(jnp.logical_not(early))(expand_own)
 
     def add(k, a, out, tiles, first_tile=0):
         for ch in range(CH):
             for i, t in enumerate(tiles):
                 lanes = 128 * (first_tile + i)
                 out[ch, t] += a[R[k] * ch : R[k] * (ch + 1), lanes : lanes + 128]
-
-    for m in (6, 7):
-        pl.when(there(-messages[m][2], -messages[m][3]))(copies[m].wait_recv)
-    sub = lax.broadcasted_iota(jnp.int32, (8, 512), 0)
-    terms = [a.astype(F32) for a in split3(jnp.where(sub < 3, cbm[...], cbp[...]))]
-    came = jnp.concatenate(
-        [of_level(k, a) for k in range(1, LEVELS + 1) for a in terms] + [jnp.zeros((8, 512), F32)], axis=0
-    )
-    came = jnp.transpose(came)
-
-    def arrived(k, at, rows, lanes, count):
-        return jnp.dot(
-            came[at : at + rows].astype(BF16), arrive[:, lanes : lanes + count], preferred_element_type=F32
-        )[BASE[k] - at :]
-
-    more = arrived(1, 0, 224, 0, 512)
-    add(1, more, g1, (0, 3))
-    add(1, more, m1, (0, 1), 2)
-    more = arrived(2, 208, 128, 512, 384)
-    add(2, more, g2, (0, 1))
-    add(2, more, m2, (0,), 2)
-    for k, at, g, m in deeper:
-        more = arrived(k, BASE[3] + at, 16 * -(-3 * R[k] // 16), 896 + 256 * (k - 3), 256)
-        add(k, more, g, (0,))
-        add(k, more, m, (0,), 1)
 
     side = jnp.bitwise_and(lane, 7) < 3
     middle = jnp.logical_and(lane >= 64, lane < 104)
@@ -419,6 +407,31 @@
     for m in (3, 4, 5):
         pl.when(there(-messages[m][2], -messages[m][3]))(copies[m].wait_recv)
     add_rows(rl_in, clm, clp, 2, lambda k: H[k] - 1)
+    for m in (6, 7):
+        pl.when(there(-messages[m][2], -messages[m][3]))(copies[m].wait_recv)
+    sub = lax.broadcasted_iota(jnp.int32, (8, 512), 0)
+    terms = [a.astype(F32) for a in split3(jnp.where(sub < 3, cbm[...], cbp[...]))]
+    came = jnp.concatenate(
+        [of_level(k, a) for k in range(1, LEVELS + 1) for a in terms] + [jnp.zeros((8, 512), F32)], axis=0
+    )
+    came = jnp.transpose(came)
+
+    def arrived(k, at, rows, lanes, count):
+        return jnp.dot(
+            came[at : at + rows].astype(BF16), arrive[:, lanes : lanes + count], preferred_element_type=F32
+        )[BASE[k] - at :]
+
+    more = arrived(1, 0, 224, 0, 512)
+    add(1, more, g1, (0, 3))
+    add(1, more, m1, (0, 1), 2)
+    more = arrived(2, 208, 128, 512, 384)
+    add(2, more, g2, (0, 1))
+    add(2, more, m2, (0,), 2)
+    for k, at, g, m in deeper:
+        more = arrived(k, BASE[3] + at, 16 * -(-3 * R[k] // 16), 896 + 256 * (k - 3), 256)
+        add(k, more, g, (0,))
+        add(k, more, m, (0,), 1)
+
     for k, g in enumerate((g1, g2, g3, g4, g5), 1):
         g[:, :, H[k] + 1 : H[k] + 2, :] = g[:, :, pl.ds(jnp.where(last, H[k], H[k] + 1), 1), :]
     details(H[1:6])

time: 14.2 us -> 13.1 us (0.923)
  Pallas kernels: 13.4 us -> 12.3 us
    pallas_call x1, Pallas kernels: 12.3 us -> 11.3 us  [body(): pl.pallas_call(exchange_kernel, out_shape=[jax.ShapeDtypeStruct(shape, F3...]
where the time goes in v6:
time: 13.1 us; the launch traced here: 13 us
  Pallas kernels  12.3 us (94%)
  between operations  0.64 us (5%)
    pallas_call x1, Pallas kernels, body(): pl.pallas_call(exchange_kernel, out_shape=[jax.ShapeDtypeStruct(shape, F3...  11.3 us
    pallas_call x1, Pallas kernels, body(): pl.pallas_call(result_kernel, out_shape=[jax.ShapeDtypeStruct((CH, H[k],...  1.04 us

profile of v6, /device:TPU:25, one launch (start us, length us, event | category | flops | bytes accessed | tf_op | source)
XLA Modules:
  0.0 13.0 jit_solution(9916214107807123300)
XLA Ops:
  0.6 11.3 %shard_map.136 = (f32[3,4,128,128]{3,2,1,0:T(8,128)S(1)}, f32[3,2,64,128]{3,2,1,0:T(8,128)S(1)}, f32[3,1,32,128]{3,2,1,0:T(8,128)S(1)}, f32[3,16,64]{2,1,0:T(8,1...) custom-call(f32[3,128,512]{2,1,0:T(8,128)} %x_hbm.1, bf16[2,128,1024]{2,1,0:T(8,128)(2,1)} %constant.16.clone.tlow_hbm, ...), custom_call_target="tpu_custom_call" | custom-call | tf_op jit(solution)/shard_map/pallas_call | solution.py:477
  11.9 1.0 %shard_map.137 = (f32[3,128,512]{2,1,0:T(8,128)}, f32[3,64,256]{2,1,0:T(8,128)}, f32[3,32,128]{2,1,0:T(8,128)}, f32[3,16,64]{2,1,0:T(8,128)}, f32[3,8,32]{2,1,0:T(8,128)}, /*index=5*/f32[3,4,16]{2,1,0:T(4,128)}) custom-call(f32[3,4,128,128]{3,2,1,0:T(8,128)S(1)} %get-tuple-element.12.d0, f32[3,2,64,128]{3,2,1,0:T(8,128)S(1)} %get-tuple-element.13.d1, ...), custom_call_target="tpu_custom_call" | custom-call | tf_op jit(solution)/shard_map/pallas_call | solution.py:485

commit v7 on v6

--- a/solution.py
+++ b/solution.py
@@ -197,10 +197,16 @@
     up, down = jnp.logical_not(first), jnp.logical_not(last)
     west, east = jnp.logical_not(left), jnp.logical_not(right)
 
-    loads = [
-        pltpu.make_async_copy(x_hbm.at[:, :, pl.ds(128 * t, 128)], xs.at[:, t, pl.ds(8, ROWS), :], load_sem.at[t])
-        for t in range(4)
-    ]
+    def image(at, rows, sem):
+        return [
+            pltpu.make_async_copy(
+                x_hbm.at[:, pl.ds(at, rows), pl.ds(128 * t, 128)], xs.at[:, t, pl.ds(8 + at, rows), :], load_sem.at[sem + t]
+            )
+            for t in range(4)
+        ]
+
+    loads = image(32, ROWS - 32, 0)
+    upper = image(0, 32, 12)
     loads += [
         pltpu.make_async_copy(tlow_hbm.at[left.astype(jnp.int32)], tv.at[pl.ds(0, 128)], load_sem.at[4]),
         pltpu.make_async_copy(tmid_hbm, tv.at[pl.ds(128, 256)], load_sem.at[5]),
@@ -211,7 +217,7 @@
         pltpu.make_async_copy(w345_hbm, w345, load_sem.at[10]),
         pltpu.make_async_copy(arrive_hbm, arrive, load_sem.at[11]),
     ]
-    for copy in loads[:7]:
+    for copy in loads[:4]:
         copy.start()
 
     def there(dr, dc):
@@ -243,6 +249,9 @@
         def _(dst=dst):
             dst[...] = jnp.zeros_like(dst)
 
+    for copy in loads[4:7] + upper:
+        copy.start()
+
     ys = (xs, y1, y2, y3, y4, y5)
     for k in range(LEVELS):
         ys[k][:, :, 0:8, :] = jnp.zeros((CH, 4, 8, 128), F32)
@@ -255,14 +264,15 @@
     for copy in loads[:4]:
         copy.wait()
     for k in range(1, LEVELS + 1):
+        if k == 3:
+            for copy in loads[4:7]:
+                copy.wait()
         mirror_end(ys[k - 1], H[k - 1], last)
         for t in range(4):
             reduce_rows(t, ys[k - 1], ys[k], BELOW[k])
         for ch in range(CH):
             at = 16 * (k - 1) + 3 * ch
             srs[:, at : at + 3, :] = ys[k][ch, :, 7 + H[k] : 10 + H[k], :]
-    for copy in loads[4:7]:
-        copy.wait()
     lane = lax.broadcasted_iota(jnp.int32, (16, 128), 1)
 
     def form_strips(out, corners, count):
@@ -297,6 +307,8 @@
     deeper = ((3, 0, g3, m3), (4, 72, g4, m4), (5, 112, g5, m5))
 
     def reduce_rest():
+        for copy in upper:
+            copy.wait()
         for k in range(1, LEVELS + 1):
             mirror_start(ys[k - 1], first)
             for t in range(4):
@@ -470,7 +482,7 @@
     scratch += [vmem(CH, t, R[k], 128) for k, t in ((1, 4), (2, 2), (3, 1), (4, 1), (5, 1))]
     scratch += [vmem(CH, t, R[k], 128) for k, t in ((1, 2), (2, 1), (3, 1), (4, 1), (5, 1))]
     scratch += [vmem(CH, 1, H[3], 128), vmem(CH, 1, H[4], 128)]
-    scratch += [pltpu.SemaphoreType.DMA((n,)) for n in (12, 8, 8)]
+    scratch += [pltpu.SemaphoreType.DMA((n,)) for n in (16, 8, 8)]
     far = pl.BlockSpec(memory_space=pltpu.HBM)
     inside = pl.BlockSpec(memory_space=pltpu.VMEM)
     inputs = [pltpu.with_memory_space_constraint(jnp.asarray(a), pltpu.HBM) for a in (orthophoto, *tables())]

time: 13.1 us -> 13.2 us (level)
  no operation moved by 1% of the time
where the time goes in v7:
time: 13.2 us; the launch traced here: 13 us
  Pallas kernels  12.4 us (94%)
  between operations  0.64 us (5%)
    pallas_call x1, Pallas kernels, body(): pl.pallas_call(exchange_kernel, out_shape=[jax.ShapeDtypeStruct(shape, F3...  11.4 us
    pallas_call x1, Pallas kernels, body(): pl.pallas_call(result_kernel, out_shape=[jax.ShapeDtypeStruct((CH, H[k],...  1.04 us

profile of v7, /device:TPU:25, one launch (start us, length us, event | category | flops | bytes accessed | tf_op | source)
XLA Modules:
  0.0 13.0 jit_solution(4907902305368139506)
XLA Ops:
  0.6 11.4 %shard_map.136 = (f32[3,4,128,128]{3,2,1,0:T(8,128)S(1)}, f32[3,2,64,128]{3,2,1,0:T(8,128)S(1)}, f32[3,1,32,128]{3,2,1,0:T(8,128)S(1)}, f32[3,16,64]{2,1,0:T(8,1...) custom-call(f32[3,128,512]{2,1,0:T(8,128)} %x_hbm.1, bf16[2,128,1024]{2,1,0:T(8,128)(2,1)} %constant.16.clone.tlow_hbm, ...), custom_call_target="tpu_custom_call" | custom-call | tf_op jit(solution)/shard_map/pallas_call | solution.py:489
  12.0 1.0 %shard_map.137 = (f32[3,128,512]{2,1,0:T(8,128)}, f32[3,64,256]{2,1,0:T(8,128)}, f32[3,32,128]{2,1,0:T(8,128)}, f32[3,16,64]{2,1,0:T(8,128)}, f32[3,8,32]{2,1,0:T(8,128)}, /*index=5*/f32[3,4,16]{2,1,0:T(4,128)}) custom-call(f32[3,4,128,128]{3,2,1,0:T(8,128)S(1)} %get-tuple-element.12.d0, f32[3,2,64,128]{3,2,1,0:T(8,128)S(1)} %get-tuple-element.13.d1, ...), custom_call_target="tpu_custom_call" | custom-call | tf_op jit(solution)/shard_map/pallas_call | solution.py:497

commit v8 on v7

--- a/solution.py
+++ b/solution.py
@@ -52,21 +52,23 @@
         a[:, at + 8 * (k - 1) : at + 8 * (k - 1) + 5] = t[k][:, [c + 1 for c in cells]]
         a[:, at + 112 + 2 * (k - 1) : at + 114 + 2 * (k - 1)] = t[k][:, [beyond + 1, before + 1]]
 
-    first = np.zeros((COLS, 512))
-    first[:, 0:256] = t[1][:, 1:257]
-    first[:, 384:512] = t[2][:, 1:129]
-    last = np.zeros((COLS, 256))
-    for k in (3, 4, 5):
-        fill(last, 0, k)
-        last[:, 128 + POS[k] : 128 + POS[k] + W[k]] = t[k][:, 1 : W[k] + 1]
-    for k in (1, 2):
-        fill(first, 256, k)
-    top = np.asarray(last.astype(jnp.bfloat16), np.float64)
-    rest = np.asarray((last - top).astype(jnp.bfloat16), np.float64)
-    assert np.array_equal(top + rest, last)
-    first[:, 272:296] = top[:, 16:40]
-    assert np.array_equal(np.asarray(first.astype(jnp.bfloat16), np.float64), first)
-    return np.concatenate([first, top, rest], axis=1)
+    near = np.zeros((COLS, 384))
+    near[:, 0:256] = t[1][:, 1:257]
+    near[:, 256:384] = t[2][:, 1:129]
+    deep, cells = np.zeros((COLS, 128)), np.zeros((COLS, 128))
+    for k in range(1, LEVELS + 1):
+        fill(cells, 0, k)
+        if k > 2:
+            deep[:, POS[k] : POS[k] + W[k]] = t[k][:, 1 : W[k] + 1]
+    assert not cells[128:384].any()
+    return np.concatenate([near, *two_terms(deep)], axis=1), np.concatenate(two_terms(cells), axis=1)
+
+
+def two_terms(a):
+    top = np.asarray(a.astype(jnp.bfloat16), np.float64)
+    rest = np.asarray((a - top).astype(jnp.bfloat16), np.float64)
+    assert np.array_equal(top + rest, a)
+    return top, rest
 
 
 def expansion_row(k, cell):
@@ -111,10 +113,15 @@
 
 
 def tables():
-    plain, low, high = (reduction_table(*e) for e in ((False, False), (True, False), (False, True)))
+    (plain, cells), (low, cells_low), (high, cells_high) = (
+        reduction_table(*e) for e in ((False, False), (True, False), (False, True))
+    )
     assert np.array_equal(plain[128:], low[128:]) and np.array_equal(plain[:384], high[:384])
+    assert np.array_equal(plain[:, 0:384], np.asarray(plain[:, 0:384].astype(jnp.bfloat16), np.float64))
     t_low = np.stack([plain[:128], low[:128]])
     t_high = np.stack([plain[384:], high[384:]])
+    c_low = np.stack([cells[:128], cells_low[:128]])
+    c_high = np.stack([cells[384:], cells_high[384:]])
     v1, s1 = expansion_table(1, 0, 256, 384)
     w2 = np.concatenate(expansion_table(2, 128, 0, 256), axis=1)
     deep = []
@@ -127,7 +134,7 @@
     arrive += arrival_table(2)
     for k in (3, 4, 5):
         arrive += [padded(a, 128) for a in arrival_table(k)]
-    parts = (t_low, plain[128:384], t_high, v1, s1[256:], w2, np.stack(deep), np.concatenate(arrive, axis=1))
+    parts = (c_low, c_high, t_low, plain[128:384], t_high, v1, s1[256:], w2, np.stack(deep), np.concatenate(arrive, axis=1))
     return [a.astype(jnp.bfloat16) for a in parts]
 
 
@@ -164,8 +171,8 @@
         a[:, t, 6:7, :] = a[:, t, pl.ds(jnp.where(first, 10, 6), 1), :]
 
 
-def mirror_end(a, h, last):
-    for t in range(4):
+def mirror_end(a, tiles, h, last):
+    for t in tiles:
         a[:, t, 8 + h : 9 + h, :] = a[:, t, pl.ds(jnp.where(last, 6 + h, 8 + h), 1), :]
 
 
@@ -183,9 +190,9 @@
 
 
 def exchange_kernel(
-    x_hbm, tlow_hbm, tmid_hbm, thigh_hbm, v1_hbm, s1_hbm, w2_hbm, w345_hbm, arrive_hbm,
+    x_hbm, clow_hbm, chigh_hbm, tlow_hbm, tmid_hbm, thigh_hbm, v1_hbm, s1_hbm, w2_hbm, w345_hbm, arrive_hbm,
     d0, d1, d2, d3, d4, d5,
-    xs, y1, y2, y3, y4, y5, tv, v1, s1, w2, w345, arrive, srs, ci,
+    xs, y1, y2, y3, y4, y5, tc, co, tv, v1, s1, w2, w345, arrive, srs, ci, beside,
     rh, rl, kh, kl, cb, rh_in, rl_in, cbm, cbp, chm, chp, clm, clp,
     g1, g2, g3, g4, g5, m1, m2, m3, m4, m5, d3w, d4w,
     load_sem, send_sem, recv_sem,
@@ -205,19 +212,26 @@
             for t in range(4)
         ]
 
-    loads = image(32, ROWS - 32, 0)
-    upper = image(0, 32, 12)
-    loads += [
-        pltpu.make_async_copy(tlow_hbm.at[left.astype(jnp.int32)], tv.at[pl.ds(0, 128)], load_sem.at[4]),
-        pltpu.make_async_copy(tmid_hbm, tv.at[pl.ds(128, 256)], load_sem.at[5]),
-        pltpu.make_async_copy(thigh_hbm.at[right.astype(jnp.int32)], tv.at[pl.ds(384, 128)], load_sem.at[6]),
-        pltpu.make_async_copy(v1_hbm, v1, load_sem.at[7]),
-        pltpu.make_async_copy(s1_hbm, s1, load_sem.at[8]),
-        pltpu.make_async_copy(w2_hbm, w2, load_sem.at[9]),
-        pltpu.make_async_copy(w345_hbm, w345, load_sem.at[10]),
-        pltpu.make_async_copy(arrive_hbm, arrive, load_sem.at[11]),
+    lower = image(32, ROWS - 32, 0)
+    upper = image(0, 32, 4)
+    at_left, at_right = left.astype(jnp.int32), right.astype(jnp.int32)
+    cell_tables = [
+        pltpu.make_async_copy(clow_hbm.at[at_left], tc.at[pl.ds(0, 128)], load_sem.at[8]),
+        pltpu.make_async_copy(chigh_hbm.at[at_right], tc.at[pl.ds(128, 128)], load_sem.at[9]),
     ]
-    for copy in loads[:4]:
+    row_tables = [
+        pltpu.make_async_copy(tlow_hbm.at[at_left], tv.at[pl.ds(0, 128)], load_sem.at[10]),
+        pltpu.make_async_copy(tmid_hbm, tv.at[pl.ds(128, 256)], load_sem.at[11]),
+        pltpu.make_async_copy(thigh_hbm.at[at_right], tv.at[pl.ds(384, 128)], load_sem.at[12]),
+    ]
+    own_tables = [
+        pltpu.make_async_copy(v1_hbm, v1, load_sem.at[13]),
+        pltpu.make_async_copy(s1_hbm, s1, load_sem.at[14]),
+        pltpu.make_async_copy(w2_hbm, w2, load_sem.at[15]),
+        pltpu.make_async_copy(w345_hbm, w345, load_sem.at[16]),
+        pltpu.make_async_copy(arrive_hbm, arrive, load_sem.at[17]),
+    ]
+    for copy in (lower[0], lower[3], *cell_tables, lower[1], lower[2], *row_tables):
         copy.start()
 
     def there(dr, dc):
@@ -249,7 +263,7 @@
         def _(dst=dst):
             dst[...] = jnp.zeros_like(dst)
 
-    for copy in loads[4:7] + upper:
+    for copy in upper:
         copy.start()
 
     ys = (xs, y1, y2, y3, y4, y5)
@@ -261,38 +275,47 @@
     for a in (rh, kh, kl):
         a[...] = jnp.zeros_like(a)
 
-    for copy in loads[:4]:
-        copy.wait()
-    for k in range(1, LEVELS + 1):
-        if k == 3:
-            for copy in loads[4:7]:
-                copy.wait()
-        mirror_end(ys[k - 1], H[k - 1], last)
-        for t in range(4):
-            reduce_rows(t, ys[k - 1], ys[k], BELOW[k])
-        for ch in range(CH):
-            at = 16 * (k - 1) + 3 * ch
-            srs[:, at : at + 3, :] = ys[k][ch, :, 7 + H[k] : 10 + H[k], :]
     lane = lax.broadcasted_iota(jnp.int32, (16, 128), 1)
 
-    def form_strips(out, corners, count):
-        strips = jnp.concatenate([srs[t] for t in range(4)], axis=1)
-        near = dot3(strips[0:32], tv[:, 0:512])
-        deep = dot3(strips[32:80], tv[:, 512:1024])
-        deep = deep[:, 0:256] + deep[:, 256:512]
-        cells = jnp.where(lane < 32, deep[16:32, 0:128], deep[32:48, 0:128])
-        cells = jnp.where(lane < 24, deep[0:16, 0:128], cells)
-        cells = jnp.where(lane < 8, near[0:16, 256:384], jnp.where(lane < 16, near[16:32, 256:384], cells))
-        beside = jnp.where(lane < 118, deep[0:16, 0:128], jnp.where(lane < 120, deep[16:32, 0:128], deep[32:48, 0:128]))
-        beside = jnp.where(lane < 114, near[0:16, 256:384], jnp.where(lane < 116, near[16:32, 256:384], beside))
-        small = jnp.where(lane < 96, deep[16:32, 128:256], deep[32:48, 128:256])
-        small = jnp.where(lane < 64, deep[0:16, 128:256], jnp.where(lane < 112, small, beside))
-        for t, a in enumerate((near[0:16, 0:128], near[0:16, 128:256], near[16:32, 384:512], small)):
-            out[pl.ds(t, CH * count, stride=4), :] = a[0 : CH * count]
+    def reduce_lower(tiles):
+        for k in range(1, LEVELS + 1):
+            mirror_end(ys[k - 1], tiles, H[k - 1], last)
+            for t in tiles:
+                reduce_rows(t, ys[k - 1], ys[k], BELOW[k])
+            for ch in range(CH):
+                at = 16 * (k - 1) + 3 * ch
+                for t in tiles:
+                    srs[t, at : at + 3, :] = ys[k][ch, t, 7 + H[k] : 10 + H[k], :]
+
+    def form_corners(corners, count):
+        both = dot3(jnp.concatenate([srs[0], srs[3]], axis=1), tc[...])
+        both = both[:, 0:128] + both[:, 128:256]
+        level = [both[16 * k : 16 * k + 16] for k in range(LEVELS)]
+        cells, halo = level[4], level[4]
+        for k in (3, 2, 1, 0):
+            cells = jnp.where(lane < 8 * k + 8, level[k], cells)
+            halo = jnp.where(lane < 114 + 2 * k, level[k], halo)
+        beside[...] = halo
         ci[...] = jnp.where(lane < 40, cells, 0.0)
         corners[0:3, :] = sum(pltpu.roll(ci[pl.ds(i, CH, stride=count), :], 40 * i, 1) for i in range(count))
 
-    form_strips(rh, kh, 3)
+    def form_strips(out, count):
+        strips = jnp.concatenate([srs[t] for t in range(4)], axis=1)
+        near = dot3(strips[0:32], tv[:, 0:384])
+        deep = dot3(strips[32:80], tv[:, 384:640])
+        deep = deep[:, 0:128] + deep[:, 128:256]
+        small = jnp.where(lane < 96, deep[16:32], deep[32:48])
+        small = jnp.where(lane < 64, deep[0:16], jnp.where(lane < 112, small, beside[...]))
+        for t, a in enumerate((near[0:16, 0:128], near[0:16, 128:256], near[16:32, 256:384], small)):
+            out[pl.ds(t, CH * count, stride=4), :] = a[0 : CH * count]
+
+    for copy in (lower[0], lower[3]):
+        copy.wait()
+    reduce_lower((0, 3))
+    for copy in cell_tables:
+        copy.wait()
+    form_corners(kh, 3)
+
     place = lax.broadcasted_iota(jnp.int32, (8, 512), 1)
 
     def of_level(k, a):
@@ -318,38 +341,50 @@
             for ch in range(CH):
                 at = 16 * (k - 1) + 2 * ch
                 srs[:, at : at + 2, :] = ys[k][ch, :, 7:9, :]
-        form_strips(rl, kl, 2)
+        form_corners(kl, 2)
+        form_strips(rl, 2)
         outer = jnp.concatenate([rows_of(k, ys[k], (0, 3)) for k in range(1, LEVELS + 1)], axis=0)
-        table = jnp.concatenate([tv[0:128], tv[384:512]], axis=0)
-        turned = dot3(outer, jnp.concatenate([table[:, 256:384], table[:, 768:896]], axis=1))
-        turned = jnp.concatenate([turned[:, 0:128] + turned[:, 128:256], jnp.zeros((32, 128), F32)], axis=0)
+        cells = dot3(outer, tc[...])
+        cells = cells[:, 0:128] + cells[:, 128:256]
+        co[...] = cells
+        turned = jnp.concatenate([cells, jnp.zeros((32, 128), F32)], axis=0)
         turned = jnp.transpose(turned)
         cb[...] = sum(of_level(k, turned[8 * (k - 1) : 8 * k]) for k in range(1, LEVELS + 1))
 
     def expand_own():
-        for copy in loads[7:]:
+        for copy in own_tables:
             copy.start()
-        p12 = dot3(jnp.concatenate([rows_of(k, ys[k], range(4)) for k in (1, 2)], axis=0), tv[:, 0:512])
-        p345 = dot3(jnp.concatenate([rows_of(k, ys[k], range(4)) for k in (3, 4, 5)], axis=0), tv[:, 512:1024])
-        p345 = p345[:, 0:256] + p345[:, 256:512]
-
-        for copy in loads[7:]:
+        p12 = dot3(jnp.concatenate([rows_of(k, ys[k], range(4)) for k in (1, 2)], axis=0), tv[:, 0:384])
+        p345 = dot3(jnp.concatenate([rows_of(k, ys[k], range(4)) for k in (3, 4, 5)], axis=0), tv[:, 384:640])
+        p345 = p345[:, 0:128] + p345[:, 128:256]
+        cells = co[...]
+        for copy in own_tables:
             copy.wait()
-        put(1, dot3(p12[0:224, 0:384], v1[...]), g1)
+        put(1, dot3(jnp.concatenate([p12[0:224, 0:256], cells[0:224]], axis=1), v1[...]), g1)
         put(1, p12, m1)
-        both = dot3(p12[208:336, 256:512], w2[...])
+        both = dot3(jnp.concatenate([cells[208:336], p12[208:336, 256:384]], axis=1), w2[...])
         put(2, both[8:, 0:256], g2)
         put(2, both[8:, 256:384], m2)
         for k, at, g, m in deeper:
-            both = dot3(p345[at : at + 16 * -(-3 * R[k] // 16)], w345[k - 3])
+            rows = 16 * -(-3 * R[k] // 16)
+            both = dot3(jnp.concatenate([cells[336 + at : 336 + at + rows], p345[at : at + rows]], axis=1), w345[k - 3])
             skip = BASE[k] - BASE[3] - at
             put(k, both[skip:, 0:128], g)
             put(k, both[skip:, 128:256], m)
 
     early = lax.rem(r, 8) == 0
 
+    def finish_lower():
+        for copy in (lower[1], lower[2]):
+            copy.wait()
+        reduce_lower((1, 2))
+        for copy in row_tables:
+            copy.wait()
+        form_strips(rh, 3)
+
     @pl.when(early)
     def _():
+        finish_lower()
         reduce_rest()
         expand_own()
 
@@ -365,8 +400,10 @@
                 device_id=(r + dr, c + dc), device_id_type=MESH,
             )
         )
-    for m in (1, 2, 0):
+    for m in (1, 2):
         pl.when(there(*messages[m][2:]))(copies[m].start)
+    pl.when(jnp.logical_not(early))(finish_lower)
+    pl.when(there(1, 0))(copies[0].start)
 
 
     @pl.when(jnp.logical_not(early))
@@ -473,16 +510,17 @@
     held = [(CH, 4, H[0], 128), (CH, 2, H[1], 128), (CH, 1, H[2], 128)]
     held += [(CH, H[3], W[3]), (CH, H[4], W[4]), (CH, H[5], W[5])]
     scratch = [vmem(CH, 4, H[k] + 32, 128) for k in range(6)]
-    scratch += [vmem(512, 1024, dtype=BF16), vmem(384, 512, dtype=BF16), vmem(128, 256, dtype=BF16)]
+    scratch += [vmem(256, 256, dtype=BF16), vmem(480, 128)]
+    scratch += [vmem(512, 640, dtype=BF16), vmem(384, 512, dtype=BF16), vmem(128, 256, dtype=BF16)]
     scratch += [vmem(256, 384, dtype=BF16), vmem(3, 256, 256, dtype=BF16), vmem(128, 1664, dtype=BF16)]
-    scratch += [vmem(4, 80, 128), vmem(16, 128)]
+    scratch += [vmem(4, 80, 128), vmem(16, 128), vmem(16, 128)]
     scratch += [vmem(40, 128), vmem(24, 128), vmem(4, 128), vmem(4, 128), vmem(8, 512)]
     scratch += [vmem(40, 128), vmem(24, 128), vmem(8, 512), vmem(8, 512)]
     scratch += [vmem(4, 128)] * 4
     scratch += [vmem(CH, t, R[k], 128) for k, t in ((1, 4), (2, 2), (3, 1), (4, 1), (5, 1))]
     scratch += [vmem(CH, t, R[k], 128) for k, t in ((1, 2), (2, 1), (3, 1), (4, 1), (5, 1))]
     scratch += [vmem(CH, 1, H[3], 128), vmem(CH, 1, H[4], 128)]
-    scratch += [pltpu.SemaphoreType.DMA((n,)) for n in (16, 8, 8)]
+    scratch += [pltpu.SemaphoreType.DMA((n,)) for n in (18, 8, 8)]
     far = pl.BlockSpec(memory_space=pltpu.HBM)
     inside = pl.BlockSpec(memory_space=pltpu.VMEM)
     inputs = [pltpu.with_memory_space_constraint(jnp.asarray(a), pltpu.HBM) for a in (orthophoto, *tables())]

time: 13.2 us -> 12.8 us (0.970)
  Pallas kernels: 12.4 us -> 12 us
    pallas_call x1, Pallas kernels: 11.4 us -> 11 us  [body(): pl.pallas_call(exchange_kernel, out_shape=[jax.ShapeDtypeStruct(shape, F3...]
where the time goes in v8:
time: 12.8 us; the launch traced here: 12.7 us
  Pallas kernels  12 us (94%)
  between operations  0.64 us (5%)
    pallas_call x1, Pallas kernels, body(): pl.pallas_call(exchange_kernel, out_shape=[jax.ShapeDtypeStruct(shape, F3...  11 us
    pallas_call x1, Pallas kernels, body(): pl.pallas_call(result_kernel, out_shape=[jax.ShapeDtypeStruct((CH, H[k],...  1.04 us

profile of v8, /device:TPU:25, one launch (start us, length us, event | category | flops | bytes accessed | tf_op | source)
XLA Modules:
  0.0 12.7 jit_solution(10060635842336080062)
XLA Ops:
  0.6 11.0 %shard_map.154 = (f32[3,4,128,128]{3,2,1,0:T(8,128)S(1)}, f32[3,2,64,128]{3,2,1,0:T(8,128)S(1)}, f32[3,1,32,128]{3,2,1,0:T(8,128)S(1)}, f32[3,16,64]{2,1,0:T(8,1...) custom-call(f32[3,128,512]{2,1,0:T(8,128)} %x_hbm.1, bf16[2,128,256]{2,1,0:T(8,128)(2,1)} %constant.20.clone.clow_hbm, ...), custom_call_target="tpu_custom_call" | custom-call | tf_op jit(solution)/shard_map/pallas_call | solution.py:527
  11.6 1.0 %shard_map.155 = (f32[3,128,512]{2,1,0:T(8,128)}, f32[3,64,256]{2,1,0:T(8,128)}, f32[3,32,128]{2,1,0:T(8,128)}, f32[3,16,64]{2,1,0:T(8,128)}, f32[3,8,32]{2,1,0:T(8,128)}, /*index=5*/f32[3,4,16]{2,1,0:T(4,128)}) custom-call(f32[3,4,128,128]{3,2,1,0:T(8,128)S(1)} %get-tuple-element.12.d0, f32[3,2,64,128]{3,2,1,0:T(8,128)S(1)} %get-tuple-element.13.d1, ...), custom_call_target="tpu_custom_call" | custom-call | tf_op jit(solution)/shard_map/pallas_call | solution.py:535

commit v9 on v8

--- a/solution.py
+++ b/solution.py
@@ -372,7 +372,8 @@
             put(k, both[skip:, 0:128], g)
             put(k, both[skip:, 128:256], m)
 
-    early = lax.rem(r, 8) == 0
+    z = lax.rem(r, 8)
+    early, earliest = z < 4, z == 0
 
     def finish_lower():
         for copy in (lower[1], lower[2]):
@@ -386,7 +387,8 @@
     def _():
         finish_lower()
         reduce_rest()
-        expand_own()
+
+    pl.when(earliest)(expand_own)
 
     neighbours = (up.astype(jnp.int32) + down.astype(jnp.int32) + 1) * (
         west.astype(jnp.int32) + east.astype(jnp.int32) + 1
@@ -412,7 +414,7 @@
 
     for m in range(3, 8):
         pl.when(there(*messages[m][2:]))(copies[m].start)
-    pl.when(jnp.logical_not(early))(expand_own)
+    pl.when(jnp.logical_not(earliest))(expand_own)
 
     def add(k, a, out, tiles, first_tile=0):
         for ch in range(CH):

time: 12.8 us -> 12.8 us (level)
  no operation moved by 1% of the time
where the time goes in v9:
time: 12.8 us; the launch traced here: 12.7 us
  Pallas kernels  12 us (94%)
  between operations  0.64 us (5%)
    pallas_call x1, Pallas kernels, body(): pl.pallas_call(exchange_kernel, out_shape=[jax.ShapeDtypeStruct(shape, F3...  11 us
    pallas_call x1, Pallas kernels, body(): pl.pallas_call(result_kernel, out_shape=[jax.ShapeDtypeStruct((CH, H[k],...  1.04 us

profile of v9, /device:TPU:25, one launch (start us, length us, event | category | flops | bytes accessed | tf_op | source)
XLA Modules:
  0.0 12.7 jit_solution(5025915787030186761)
XLA Ops:
  0.6 11.0 %shard_map.154 = (f32[3,4,128,128]{3,2,1,0:T(8,128)S(1)}, f32[3,2,64,128]{3,2,1,0:T(8,128)S(1)}, f32[3,1,32,128]{3,2,1,0:T(8,128)S(1)}, f32[3,16,64]{2,1,0:T(8,1...) custom-call(f32[3,128,512]{2,1,0:T(8,128)} %x_hbm.1, bf16[2,128,256]{2,1,0:T(8,128)(2,1)} %constant.20.clone.clow_hbm, ...), custom_call_target="tpu_custom_call" | custom-call | tf_op jit(solution)/shard_map/pallas_call | solution.py:529
  11.6 1.0 %shard_map.155 = (f32[3,128,512]{2,1,0:T(8,128)}, f32[3,64,256]{2,1,0:T(8,128)}, f32[3,32,128]{2,1,0:T(8,128)}, f32[3,16,64]{2,1,0:T(8,128)}, f32[3,8,32]{2,1,0:T(8,128)}, /*index=5*/f32[3,4,16]{2,1,0:T(4,128)}) custom-call(f32[3,4,128,128]{3,2,1,0:T(8,128)S(1)} %get-tuple-element.12.d0, f32[3,2,64,128]{3,2,1,0:T(8,128)S(1)} %get-tuple-element.13.d1, ...), custom_call_target="tpu_custom_call" | custom-call | tf_op jit(solution)/shard_map/pallas_call | solution.py:537

commit v10 on v9

--- a/solution.py
+++ b/solution.py
@@ -231,7 +231,7 @@
         pltpu.make_async_copy(w345_hbm, w345, load_sem.at[16]),
         pltpu.make_async_copy(arrive_hbm, arrive, load_sem.at[17]),
     ]
-    for copy in (lower[0], lower[3], *cell_tables, lower[1], lower[2], *row_tables):
+    for copy in (*lower, *cell_tables, *row_tables):
         copy.start()
 
     def there(dr, dc):
@@ -279,6 +279,9 @@
 
     def reduce_lower(tiles):
         for k in range(1, LEVELS + 1):
+            if k == 3:
+                for copy in cell_tables + row_tables:
+                    copy.wait()
             mirror_end(ys[k - 1], tiles, H[k - 1], last)
             for t in tiles:
                 reduce_rows(t, ys[k - 1], ys[k], BELOW[k])
@@ -309,12 +312,11 @@
         for t, a in enumerate((near[0:16, 0:128], near[0:16, 128:256], near[16:32, 256:384], small)):
             out[pl.ds(t, CH * count, stride=4), :] = a[0 : CH * count]
 
-    for copy in (lower[0], lower[3]):
+    for copy in lower:
         copy.wait()
-    reduce_lower((0, 3))
-    for copy in cell_tables:
-        copy.wait()
+    reduce_lower(range(4))
     form_corners(kh, 3)
+    form_strips(rh, 3)
 
     place = lax.broadcasted_iota(jnp.int32, (8, 512), 1)
 
@@ -375,19 +377,7 @@
     z = lax.rem(r, 8)
     early, earliest = z < 4, z == 0
 
-    def finish_lower():
-        for copy in (lower[1], lower[2]):
-            copy.wait()
-        reduce_lower((1, 2))
-        for copy in row_tables:
-            copy.wait()
-        form_strips(rh, 3)
-
-    @pl.when(early)
-    def _():
-        finish_lower()
-        reduce_rest()
-
+    pl.when(early)(reduce_rest)
     pl.when(earliest)(expand_own)
 
     neighbours = (up.astype(jnp.int32) + down.astype(jnp.int32) + 1) * (
@@ -402,10 +392,8 @@
                 device_id=(r + dr, c + dc), device_id_type=MESH,
             )
         )
-    for m in (1, 2):
+    for m in (1, 2, 0):
         pl.when(there(*messages[m][2:]))(copies[m].start)
-    pl.when(jnp.logical_not(early))(finish_lower)
-    pl.when(there(1, 0))(copies[0].start)
 
 
     @pl.when(jnp.logical_not(early))

time: 12.8 us -> 13 us (1.016)
  Pallas kernels: 12 us -> 12.2 us
    pallas_call x1, Pallas kernels: 11 us -> 11.2 us  [body(): pl.pallas_call(exchange_kernel, out_shape=[jax.ShapeDtypeStruct(shape, F3...]
where the time goes in v10:
time: 13 us; the launch traced here: 12.9 us
  Pallas kernels  12.2 us (94%)
  between operations  0.64 us (5%)
    pallas_call x1, Pallas kernels, body(): pl.pallas_call(exchange_kernel, out_shape=[jax.ShapeDtypeStruct(shape, F3...  11.2 us
    pallas_call x1, Pallas kernels, body(): pl.pallas_call(result_kernel, out_shape=[jax.ShapeDtypeStruct((CH, H[k],...  1.04 us

profile of v10, /device:TPU:25, one launch (start us, length us, event | category | flops | bytes accessed | tf_op | source)
XLA Modules:
  0.0 12.9 jit_solution(6001567497015389868)
XLA Ops:
  0.6 11.2 %shard_map.154 = (f32[3,4,128,128]{3,2,1,0:T(8,128)S(1)}, f32[3,2,64,128]{3,2,1,0:T(8,128)S(1)}, f32[3,1,32,128]{3,2,1,0:T(8,128)S(1)}, f32[3,16,64]{2,1,0:T(8,1...) custom-call(f32[3,128,512]{2,1,0:T(8,128)} %x_hbm.1, bf16[2,128,256]{2,1,0:T(8,128)(2,1)} %constant.20.clone.clow_hbm, ...), custom_call_target="tpu_custom_call" | custom-call | tf_op jit(solution)/shard_map/pallas_call | solution.py:517
  11.8 1.0 %shard_map.155 = (f32[3,128,512]{2,1,0:T(8,128)}, f32[3,64,256]{2,1,0:T(8,128)}, f32[3,32,128]{2,1,0:T(8,128)}, f32[3,16,64]{2,1,0:T(8,128)}, f32[3,8,32]{2,1,0:T(8,128)}, /*index=5*/f32[3,4,16]{2,1,0:T(4,128)}) custom-call(f32[3,4,128,128]{3,2,1,0:T(8,128)S(1)} %get-tuple-element.12.d0, f32[3,2,64,128]{3,2,1,0:T(8,128)S(1)} %get-tuple-element.13.d1, ...), custom_call_target="tpu_custom_call" | custom-call | tf_op jit(solution)/shard_map/pallas_call | solution.py:525

commit v11 on v9

--- a/solution.py
+++ b/solution.py
@@ -243,10 +243,10 @@
         return ok
 
     messages = [
-        (rh, rh_in, 1, 0),
+        (rh.at[pl.ds(0, 40)], rh_in.at[pl.ds(0, 40)], 1, 0),
         (kh, chm, 1, 1),
         (kh, chp, 1, -1),
-        (rl, rl_in, -1, 0),
+        (rl.at[pl.ds(0, 24)], rl_in.at[pl.ds(0, 24)], -1, 0),
         (kl, clm, -1, 1),
         (kl, clp, -1, -1),
         (cb, cbm, 0, 1),
@@ -288,7 +288,7 @@
                     srs[t, at : at + 3, :] = ys[k][ch, t, 7 + H[k] : 10 + H[k], :]
 
     def form_corners(corners, count):
-        both = dot3(jnp.concatenate([srs[0], srs[3]], axis=1), tc[...])
+        both = dot3(jnp.concatenate([srs[0, 0:80], srs[3, 0:80]], axis=1), tc[...])
         both = both[:, 0:128] + both[:, 128:256]
         level = [both[16 * k : 16 * k + 16] for k in range(LEVELS)]
         cells, halo = level[4], level[4]
@@ -296,11 +296,11 @@
             cells = jnp.where(lane < 8 * k + 8, level[k], cells)
             halo = jnp.where(lane < 114 + 2 * k, level[k], halo)
         beside[...] = halo
-        ci[...] = jnp.where(lane < 40, cells, 0.0)
+        ci[0:16, :] = jnp.where(lane < 40, cells, 0.0)
         corners[0:3, :] = sum(pltpu.roll(ci[pl.ds(i, CH, stride=count), :], 40 * i, 1) for i in range(count))
 
     def form_strips(out, count):
-        strips = jnp.concatenate([srs[t] for t in range(4)], axis=1)
+        strips = jnp.concatenate([srs[t, 0:80] for t in range(4)], axis=1)
         near = dot3(strips[0:32], tv[:, 0:384])
         deep = dot3(strips[32:80], tv[:, 384:640])
         deep = deep[:, 0:128] + deep[:, 128:256]
@@ -325,7 +325,7 @@
     def put(k, a, out):
         for ch in range(CH):
             for t in range(out.shape[1]):
-                out[ch, t] = a[R[k] * ch : R[k] * (ch + 1), 128 * t : 128 * (t + 1)]
+                out[ch, t, 0 : R[k], :] = a[R[k] * ch : R[k] * (ch + 1), 128 * t : 128 * (t + 1)]
 
     deeper = ((3, 0, g3, m3), (4, 72, g4, m4), (5, 112, g5, m5))
 
@@ -420,20 +420,20 @@
         for ch in range(CH):
             for i, t in enumerate(tiles):
                 lanes = 128 * (first_tile + i)
-                out[ch, t] += a[R[k] * ch : R[k] * (ch + 1), lanes : lanes + 128]
+                out[ch, t, 0 : R[k], :] += a[R[k] * ch : R[k] * (ch + 1), lanes : lanes + 128]
 
     side = jnp.bitwise_and(lane, 7) < 3
     middle = jnp.logical_and(lane >= 64, lane < 104)
     ci[...] = jnp.zeros_like(ci)
 
     def add_rows(strip, minus, plus, count, row_of):
-        corner = jnp.where(side[0:4], minus[...], plus[...])
+        corner = jnp.where(side[0:8], minus[...], plus[...])
         for i in range(count):
             ci[pl.ds(i, CH, stride=count), :] = pltpu.roll(corner, (64 - 40 * i) % 128, 1)[0:CH]
         rows = CH * count
         fill = jnp.zeros((16 - rows, 128), F32)
         tiles = [jnp.concatenate([strip[pl.ds(t, rows, stride=4), :], fill], axis=0) for t in range(4)]
-        cells = jnp.where(lane < 112, jnp.where(middle, ci[...], 0.0), tiles[3])
+        cells = jnp.where(lane < 112, jnp.where(middle, ci[0:16, :], 0.0), tiles[3])
         wide = dot3(jnp.concatenate([tiles[0], tiles[1], cells], axis=1), v1[...])
         level = jnp.concatenate(tiles[0:2], axis=1) + dot3(cells, s1[...])
         both = [dot3(jnp.concatenate([cells, tiles[2]], axis=1), w2[...])]
@@ -451,8 +451,8 @@
     def details(counts):
         for g, level, at, out, count in zip((g1, g2, g3, g4, g5), (xs, m1, m2, m3, m4), (8, 1, 1, 1, 1), (d0, d1, d2, d3w, d4w), counts):
             detail(g, level, at, out, count)
-        d3[...] = d3w[:, 0, :, 0:64]
-        d4[...] = d4w[:, 0, :, 0:32]
+        d3[...] = d3w[:, 0, 0 : H[3], 0:64]
+        d4[...] = d4w[:, 0, 0 : H[4], 0:32]
         d5[...] = m5[:, 0, 1:5, 0:16]
 
     for m in (3, 4, 5):
@@ -515,13 +515,13 @@
     scratch += [vmem(256, 256, dtype=BF16), vmem(480, 128)]
     scratch += [vmem(512, 640, dtype=BF16), vmem(384, 512, dtype=BF16), vmem(128, 256, dtype=BF16)]
     scratch += [vmem(256, 384, dtype=BF16), vmem(3, 256, 256, dtype=BF16), vmem(128, 1664, dtype=BF16)]
-    scratch += [vmem(4, 80, 128), vmem(16, 128), vmem(16, 128)]
-    scratch += [vmem(40, 128), vmem(24, 128), vmem(4, 128), vmem(4, 128), vmem(8, 512)]
-    scratch += [vmem(40, 128), vmem(24, 128), vmem(8, 512), vmem(8, 512)]
-    scratch += [vmem(4, 128)] * 4
-    scratch += [vmem(CH, t, R[k], 128) for k, t in ((1, 4), (2, 2), (3, 1), (4, 1), (5, 1))]
-    scratch += [vmem(CH, t, R[k], 128) for k, t in ((1, 2), (2, 1), (3, 1), (4, 1), (5, 1))]
-    scratch += [vmem(CH, 1, H[3], 128), vmem(CH, 1, H[4], 128)]
+    scratch += [vmem(4, 88, 128), vmem(32, 128), vmem(16, 128)]
+    scratch += [vmem(72, 128), vmem(40, 128), vmem(8, 128), vmem(8, 128), vmem(8, 512)]
+    scratch += [vmem(72, 128), vmem(40, 128), vmem(8, 512), vmem(8, 512)]
+    scratch += [vmem(8, 128)] * 4
+    scratch += [vmem(CH, t, R[k] + 8, 128) for k, t in ((1, 4), (2, 2), (3, 1), (4, 1), (5, 1))]
+    scratch += [vmem(CH, t, R[k] + 8, 128) for k, t in ((1, 2), (2, 1), (3, 1), (4, 1), (5, 1))]
+    scratch += [vmem(CH, 1, H[3] + 8, 128), vmem(CH, 1, H[4] + 8, 128)]
     scratch += [pltpu.SemaphoreType.DMA((n,)) for n in (18, 8, 8)]
     far = pl.BlockSpec(memory_space=pltpu.HBM)
     inside = pl.BlockSpec(memory_space=pltpu.VMEM)

time: 12.8 us -> 12.8 us (level)
  no operation moved by 1% of the time
where the time goes in v11:
time: 12.8 us; the launch traced here: 12.6 us
  Pallas kernels  12 us (94%)
  between operations  0.64 us (5%)
    pallas_call x1, Pallas kernels, body(): pl.pallas_call(exchange_kernel, out_shape=[jax.ShapeDtypeStruct(shape, F3...  11 us
    pallas_call x1, Pallas kernels, body(): pl.pallas_call(result_kernel, out_shape=[jax.ShapeDtypeStruct((CH, H[k],...  1.04 us

profile of v11, /device:TPU:25, one launch (start us, length us, event | category | flops | bytes accessed | tf_op | source)
XLA Modules:
  0.0 12.6 jit_solution(11319348129903007042)
XLA Ops:
  0.6 11.0 %shard_map.154 = (f32[3,4,128,128]{3,2,1,0:T(8,128)S(1)}, f32[3,2,64,128]{3,2,1,0:T(8,128)S(1)}, f32[3,1,32,128]{3,2,1,0:T(8,128)S(1)}, f32[3,16,64]{2,1,0:T(8,1...) custom-call(f32[3,128,512]{2,1,0:T(8,128)} %x_hbm.1, bf16[2,128,256]{2,1,0:T(8,128)(2,1)} %constant.20.clone.clow_hbm, ...), custom_call_target="tpu_custom_call" | custom-call | tf_op jit(solution)/shard_map/pallas_call | solution.py:529
  11.6 1.0 %shard_map.155 = (f32[3,128,512]{2,1,0:T(8,128)}, f32[3,64,256]{2,1,0:T(8,128)}, f32[3,32,128]{2,1,0:T(8,128)}, f32[3,16,64]{2,1,0:T(8,128)}, f32[3,8,32]{2,1,0:T(8,128)}, /*index=5*/f32[3,4,16]{2,1,0:T(4,128)}) custom-call(f32[3,4,128,128]{3,2,1,0:T(8,128)S(1)} %get-tuple-element.12.d0, f32[3,2,64,128]{3,2,1,0:T(8,128)S(1)} %get-tuple-element.13.d1, ...), custom_call_target="tpu_custom_call" | custom-call | tf_op jit(solution)/shard_map/pallas_call | solution.py:537

commit v12 on v11

--- a/solution.py
+++ b/solution.py
@@ -312,9 +312,10 @@
     for copy in (lower[0], lower[3]):
         copy.wait()
     reduce_lower((0, 3))
-    for copy in cell_tables:
+    for copy in (*cell_tables, lower[1], lower[2]):
         copy.wait()
     form_corners(kh, 3)
+    reduce_lower((1, 2))
 
     place = lax.broadcasted_iota(jnp.int32, (8, 512), 1)
 
@@ -376,9 +377,6 @@
     early, earliest = z < 4, z == 0
 
     def finish_lower():
-        for copy in (lower[1], lower[2]):
-            copy.wait()
-        reduce_lower((1, 2))
         for copy in row_tables:
             copy.wait()
         form_strips(rh, 3)

time: 12.8 us -> 12.9 us (level)
  no operation moved by 1% of the time
where the time goes in v12:
time: 12.9 us; the launch traced here: 12.7 us
  Pallas kernels  12.1 us (94%)
  between operations  0.64 us (5%)
    pallas_call x1, Pallas kernels, body(): pl.pallas_call(exchange_kernel, out_shape=[jax.ShapeDtypeStruct(shape, F3...  11 us
    pallas_call x1, Pallas kernels, body(): pl.pallas_call(result_kernel, out_shape=[jax.ShapeDtypeStruct((CH, H[k],...  1.04 us

profile of v12, /device:TPU:25, one launch (start us, length us, event | category | flops | bytes accessed | tf_op | source)
XLA Modules:
  0.0 12.7 jit_solution(10992111483976695620)
XLA Ops:
  0.6 11.0 %shard_map.154 = (f32[3,4,128,128]{3,2,1,0:T(8,128)S(1)}, f32[3,2,64,128]{3,2,1,0:T(8,128)S(1)}, f32[3,1,32,128]{3,2,1,0:T(8,128)S(1)}, f32[3,16,64]{2,1,0:T(8,1...) custom-call(f32[3,128,512]{2,1,0:T(8,128)} %x_hbm.1, bf16[2,128,256]{2,1,0:T(8,128)(2,1)} %constant.20.clone.clow_hbm, ...), custom_call_target="tpu_custom_call" | custom-call | tf_op jit(solution)/shard_map/pallas_call | solution.py:527
  11.7 1.0 %shard_map.155 = (f32[3,128,512]{2,1,0:T(8,128)}, f32[3,64,256]{2,1,0:T(8,128)}, f32[3,32,128]{2,1,0:T(8,128)}, f32[3,16,64]{2,1,0:T(8,128)}, f32[3,8,32]{2,1,0:T(8,128)}, /*index=5*/f32[3,4,16]{2,1,0:T(4,128)}) custom-call(f32[3,4,128,128]{3,2,1,0:T(8,128)S(1)} %get-tuple-element.12.d0, f32[3,2,64,128]{3,2,1,0:T(8,128)S(1)} %get-tuple-element.13.d1, ...), custom_call_target="tpu_custom_call" | custom-call | tf_op jit(solution)/shard_map/pallas_call | solution.py:535
